TPU v7x, 32 devices: a whole 2x2x4 slice. The times are simulated.
32 devices in a mesh: section: 2 (over x), slab: 16 (over z, y, core).
Axes of the slice: x: 2, y: 2, z: 4, core: 2. Of those that a mesh axis runs over, the one named last changes fastest.
Arguments:
- concentration: float32 [4, 2048, 2048], P('section', 'slab'), may hold values from -3.2 to 3.2
Outputs:
- new_concentration: float32 [4, 2048, 2048], P('section', 'slab')
- energy: float32 [], replicated
All inputs are finite; a program needn't handle non-finite values.
Results may differ from a plain program's by a relative error of at most 0.000098.
Values sent between devices are 32-bit elements; how exact they have to be, the bound alone decides.
A program may use at most 64 MiB of HBM per device.

v0:
```python
import functools
import math

import jax
import jax.numpy as jnp
import numpy as np
from jax import lax
from jax.experimental import pallas as pl
from jax.experimental.pallas import tpu as pltpu
from jax.sharding import PartitionSpec as P

time_step = 100.0
kappa_grad = 2.0
stabilizer = 8.0
highest = lax.Precision.HIGHEST


def circle(length, first_total, second_total, direction):
    first_index = jnp.arange(first_total, dtype=jnp.int32)
    second_index = jnp.arange(second_total, dtype=jnp.int32)
    turn_index = first_index[:, None] * second_index[None, :] % length
    phase_angle = turn_index.astype(jnp.float32) * (2.0 * math.pi / length)
    return (jnp.cos(phase_angle), direction * jnp.sin(phase_angle))


def contract(pattern, real_part, imag_part, table_cos, table_sin):

    def product_of(operand, matrix):
        return jnp.einsum(pattern, operand, matrix, precision=highest)

    out_real = product_of(real_part, table_cos) - product_of(imag_part, table_sin)
    out_imag = product_of(real_part, table_sin) + product_of(imag_part, table_cos)
    return (out_real, out_imag)


def real_only(pattern, real_part, imag_part, table_cos, table_sin):
    return jnp.einsum(pattern, real_part, table_cos, precision=highest) - jnp.einsum(
        pattern, imag_part, table_sin, precision=highest
    )


def rotate(real_part, imag_part, table_cos, table_sin):
    return (
        real_part * table_cos - imag_part * table_sin,
        real_part * table_sin + imag_part * table_cos,
    )


def wave_square(storage, length, permuted):
    if permuted:
        actual = storage // 128 + length // 128 * (storage % 128)
    else:
        actual = storage
    signed = jnp.where(2 * actual >= length, actual - length, actual)
    phase_angle = signed.astype(jnp.float32) * (2.0 * math.pi / length)
    return phase_angle * phase_angle


def plain_step(concentration):
    plane_count, row_count, full_y = concentration.shape
    slab_count = lax.axis_size("slab")
    section_count = lax.axis_size("section")
    full_x = row_count * slab_count
    full_z = plane_count * section_count
    y_block = full_y // slab_count
    y_half = y_block // section_count
    blocks_x = full_x // 128
    blocks_y = full_y // 128
    cell_count = full_x * full_y * full_z
    slab_at = lax.axis_index("slab")
    section_at = lax.axis_index("section")
    squared = concentration * concentration
    bulk_sum = jnp.sum(0.25 * squared * squared - 0.5 * squared)
    cubic_term = squared * concentration - concentration
    shaped_c = concentration.reshape(1, plane_count, row_count, blocks_y, 128)
    shaped_g = cubic_term.reshape(1, plane_count, row_count, blocks_y, 128)
    first_cos, first_sin = circle(blocks_y, blocks_y, blocks_y, -1.0)
    part_real, part_imag = contract("fzxab,aj->fzxjb", shaped_c, shaped_g, first_cos, first_sin)
    field_total = part_real.shape[0]
    twist_cos, twist_sin = circle(full_y, blocks_y, 128, -1.0)
    part_real, part_imag = rotate(part_real, part_imag, twist_cos, twist_sin)
    lane_cos, lane_sin = circle(128, 128, 128, -1.0)
    part_real, part_imag = contract("fzxjb,bk->fxjkz", part_real, part_imag, lane_cos, lane_sin)
    outgoing = jnp.concatenate([part_real, part_imag], 0).reshape(
        2 * field_total, row_count, slab_count, y_block * plane_count
    )
    columns = lax.all_to_all(outgoing, "slab", split_axis=2, concat_axis=1, tiled=True)
    columns = columns.reshape(2 * field_total, blocks_x, 128, y_block * plane_count)
    first_cos, first_sin = circle(blocks_x, blocks_x, blocks_x, -1.0)
    part_real, part_imag = contract(
        "fabm,aj->fmjb", columns[:field_total], columns[field_total:], first_cos, first_sin
    )
    twist_cos, twist_sin = circle(full_x, blocks_x, 128, -1.0)
    part_real, part_imag = rotate(part_real, part_imag, twist_cos, twist_sin)
    part_real, part_imag = contract("fmjb,bk->fmjk", part_real, part_imag, lane_cos, lane_sin)
    spectra_x = jnp.concatenate([part_real, part_imag], 0).reshape(
        2 * field_total, y_block, plane_count, full_x
    )
    depth_cos, depth_sin = circle(full_z, full_z, full_z, -1.0)
    own_cos = lax.dynamic_slice_in_dim(depth_cos, section_at * plane_count, plane_count, 0)
    own_sin = lax.dynamic_slice_in_dim(depth_sin, section_at * plane_count, plane_count, 0)
    term_real, term_imag = contract(
        "fyzk,zq->yfqk", spectra_x[:field_total], spectra_x[field_total:], own_cos, own_sin
    )
    spectral = lax.psum_scatter(
        jnp.concatenate([term_real, term_imag], 1), "section", scatter_dimension=0, tiled=True
    )
    storage_y = slab_at * y_block + section_at * y_half + jnp.arange(y_half, dtype=jnp.int32)
    storage_x = jnp.arange(full_x, dtype=jnp.int32)
    storage_z = jnp.arange(full_z, dtype=jnp.int32)
    wave_sq = (
        wave_square(storage_y, full_y, True)[:, None, None]
        + wave_square(storage_z, full_z, False)[None, :, None]
        + wave_square(storage_x, full_x, True)[None, None, :]
    )
    numerator = 1.0 + time_step * stabilizer * wave_sq
    denominator = numerator + time_step * kappa_grad * wave_sq * wave_sq
    keep_rate = numerator / denominator
    mix_rate = time_step * wave_sq / denominator
    new_real = keep_rate * spectral[:, 0] - mix_rate * spectral[:, 1]
    new_imag = keep_rate * spectral[:, 1] + mix_rate * spectral[:, 0]
    back_cos, back_sin = circle(full_z, full_z, full_z, 1.0)
    part_real, part_imag = contract("yqk,qz->yzk", new_real, new_imag, back_cos, back_sin)
    returning = jnp.stack([part_real, part_imag], 1)
    own_planes = lax.all_to_all(returning, "section", split_axis=2, concat_axis=0, tiled=True)
    grid_real = own_planes[:, 0].reshape(y_block, plane_count, blocks_x, 128)
    grid_imag = own_planes[:, 1].reshape(y_block, plane_count, blocks_x, 128)
    lane_cos, lane_sin = circle(128, 128, 128, 1.0)
    part_real, part_imag = contract("szjk,kb->szjb", grid_real, grid_imag, lane_cos, lane_sin)
    twist_cos, twist_sin = circle(full_x, blocks_x, 128, 1.0)
    part_real, part_imag = rotate(part_real, part_imag, twist_cos, twist_sin)
    first_cos, first_sin = circle(blocks_x, blocks_x, blocks_x, 1.0)
    part_real, part_imag = contract("szjb,ja->absz", part_real, part_imag, first_cos, first_sin)
    leaving = jnp.stack([part_real, part_imag], 0).reshape(2, full_x, 1, y_block * plane_count)
    rows_back = lax.all_to_all(leaving, "slab", split_axis=1, concat_axis=2, tiled=True)
    rows_back = rows_back.reshape(2, row_count, blocks_y, 128, plane_count)
    part_real, part_imag = contract("xjkz,kb->xjbz", rows_back[0], rows_back[1], lane_cos, lane_sin)
    twist_cos, twist_sin = circle(full_y, blocks_y, 128, 1.0)
    part_real, part_imag = rotate(
        part_real, part_imag, twist_cos[:, :, None], twist_sin[:, :, None]
    )
    first_cos, first_sin = circle(blocks_y, blocks_y, blocks_y, 1.0)
    new_field = real_only("xjbz,ja->zxab", part_real, part_imag, first_cos, first_sin)
    new_field = new_field.reshape(plane_count, row_count, full_y) / cell_count
    total_bulk = lax.psum(bulk_sum, ("section", "slab"))
    energy = total_bulk / cell_count
    return (new_field, energy)


lanes = 128
row_group = 32
vmem_limit = 60 * 1024 * 1024


def split(values):
    high = values.astype(jnp.bfloat16)
    low = (values - high.astype(jnp.float32)).astype(jnp.bfloat16)
    return high, low


def triple(left_parts, right_parts, dims):
    def product(left, right):
        return lax.dot_general(left, right, (dims, ((), ())), preferred_element_type=jnp.float32)

    left_high, left_low = left_parts
    right_high, right_low = right_parts
    return (
        product(left_high, right_high)
        + product(left_low, right_high)
        + product(left_high, right_low)
    )


def y_tables(full_y, devices, parity):
    half = full_y // 2
    per_part = half // 2 // devices
    slot = np.arange(half)
    device, inner = slot // (2 * per_part), slot % (2 * per_part)
    part, local = inner // per_part, inner % per_part
    wave = parity + 2 * (device * per_part + local)
    position = np.arange(half)
    turns = wave[:, None] * position[None, :] % full_y
    phase = turns * (2.0 * math.pi / full_y)
    coarse = phase[::row_group]
    offset = wave[:row_group] - wave[0]
    fine = (offset[:, None] * position[None, :] % full_y) * (2.0 * math.pi / full_y)
    fine = fine + part[:row_group, None] * (0.5 * math.pi)
    return [
        table.astype(np.float32)
        for table in (np.cos(coarse), np.sin(coarse), np.cos(fine), np.sin(fine))
    ]


def y_block(refs, block, groups, parity):
    coarse_cos, coarse_sin, fine_cos, fine_sin = refs
    cos_fine, sin_fine = fine_cos[...], fine_sin[...]
    width = cos_fine.shape[1]
    pieces = []
    for group in range(block * groups, (block + 1) * groups):
        piece = coarse_cos[group : group + 1, :] * cos_fine - coarse_sin[group : group + 1, :] * sin_fine
        if parity == 0 and group == 0:
            row = lax.broadcasted_iota(jnp.int32, piece.shape, 0)
            column = lax.broadcasted_iota(jnp.int32, piece.shape, 1)
            sign = 1.0 - 2.0 * (column % 2).astype(jnp.float32)
            piece = jnp.where(row == row_group // 2, sign, piece)
        pieces.append(piece)
    return jnp.concatenate(pieces, 0)


def forward_kernel(parity, conc_ref, ta, tb, tc, td, out_ref, high_ref, low_ref):
    planes, rows, full_y = conc_ref.shape
    half = full_y // 2
    for plane in range(planes):
        first = conc_ref[plane, :, :half]
        second = conc_ref[plane, :, half:]
        first_g = first * first * first - first
        second_g = second * second * second - second
        for field, (left, right) in enumerate(((first, second), (first_g, second_g))):
            mixed = left + right if parity == 0 else left - right
            high, low = split(mixed)
            at = (plane * 2 + field) * rows
            high_ref[at : at + rows, :] = high
            low_ref[at : at + rows, :] = low
    groups = 8
    for block in range(half // (groups * row_group)):
        table = y_block((ta, tb, tc, td), block, groups, parity)
        result = triple(split(table), (high_ref[...], low_ref[...]), ((1,), (1,)))
        out_ref[block * groups : (block + 1) * groups] = result.reshape(groups, row_group, -1)


def backward_part(parity, in_ref, tables):
    devices, inner, columns = in_ref.shape
    groups = 8
    total = None
    for block in range(devices // groups):
        at = slice(block * groups, (block + 1) * groups)
        turned = [
            in_ref[at, plane * row_group : (plane + 1) * row_group, :]
            .reshape(groups * row_group, columns)
            .T
            for plane in range(inner // row_group)
        ]
        table = y_block(tables, block, groups, parity)
        term = triple(split(jnp.concatenate(turned, 0)), split(table), ((1,), (0,)))
        total = term if total is None else total + term
    return total


def backward_even_kernel(in_ref, ta, tb, tc, td, out_ref):
    out_ref[...] = backward_part(0, in_ref, (ta, tb, tc, td))


def backward_odd_kernel(in_ref, even_ref, ta, tb, tc, td, out_ref):
    planes, rows, full_y = out_ref.shape
    half = full_y // 2
    odd = backward_part(1, in_ref, (ta, tb, tc, td))
    for plane in range(planes):
        even_rows = even_ref[plane * rows : (plane + 1) * rows, :]
        odd_rows = odd[plane * rows : (plane + 1) * rows, :]
        out_ref[plane, :, :half] = even_rows + odd_rows
        out_ref[plane, :, half:] = even_rows - odd_rows


def times_unit(real, imag, quarter_turns):
    turns = quarter_turns % 4
    if turns == 0:
        return real, imag
    if turns == 1:
        return -imag, real
    if turns == 2:
        return -real, -imag
    return imag, -real


def unit_sum(parts, power, direction):
    total_real, total_imag = parts[0]
    for index in range(1, len(parts)):
        real, imag = times_unit(*parts[index], direction * power * index)
        total_real = total_real + real
        total_imag = total_imag + imag
    return total_real, total_imag


def middle_kernel(
    has_extra, sections, in_ref, aux_ref, wx_ref, tw_cos, tw_sin, ca, sa, cb, sb, *rest
):
    if has_extra:
        part_ref, out_ref, spec_ref, fil_ref, back_ref = rest
    else:
        out_ref, spec_ref, fil_ref, back_ref = rest
    devices, inner, columns = in_ref.shape
    kk = inner // 2
    slabs = devices // sections
    zf_local = columns // lanes
    planes = zf_local // 2
    full_z = planes * sections
    quarter = slabs // 4
    width = quarter * lanes
    padded = spec_ref.shape[3]
    special = aux_ref[2, 0:8, 0:1] if has_extra else None

    def gather(section, a, part, row, zf):
        pieces = [
            in_ref[
                section * slabs + a * quarter + step,
                part * kk + row : part * kk + row + 8,
                zf * lanes : (zf + 1) * lanes,
            ]
            for step in range(quarter)
        ]
        return jnp.concatenate(pieces, 1)

    for section in range(sections):
        for zf in range(zf_local):
            at = section * zf_local + zf
            for row in range(0, padded, 8):
                source = 0 if row >= kk else row
                parts = []
                for a in range(4):
                    imag = gather(section, a, 1, source, zf)
                    if row >= kk:
                        real, imag = imag * special, jnp.zeros_like(imag)
                    else:
                        real = gather(section, a, 0, source, zf)
                        if has_extra and row == 0:
                            imag = imag * (1.0 - special)
                    parts.append((real, imag))
                for j in range(4):
                    real, imag = unit_sum(parts, j, -1)
                    if j:
                        cos, sin = tw_cos[j : j + 1, :], tw_sin[j : j + 1, :]
                        real, imag = real * cos + imag * sin, imag * cos - real * sin
                    spec_ref[j, 0, at, row : row + 8, :] = real
                    spec_ref[j, 1, at, row : row + 8, :] = imag

    cos_rows, sin_rows = [], []
    cos_fine, sin_fine = cb[...], sb[...]
    for group in range(ca.shape[0]):
        cos_base, sin_base = ca[group : group + 1, :], sa[group : group + 1, :]
        cos_rows.append(cos_base * cos_fine - sin_base * sin_fine)
        sin_rows.append(sin_base * cos_fine + cos_base * sin_fine)
    table = jnp.concatenate([jnp.concatenate(cos_rows, 0), jnp.concatenate(sin_rows, 0)], 1)
    weights = split(table)
    total_zf = sections * zf_local
    for j in range(4):
        rows = spec_ref[j].reshape(2 * total_zf * padded, width)
        raw = triple(split(rows), weights, ((1,), (0,)))
        raw = raw.reshape(2, total_zf, padded, 2 * width)
        for row in range(0, padded, 8):
            fields = []
            for field in range(2):
                per_z = []
                for z in range(full_z):
                    at = z * 2 + field
                    re_part = raw[0, at, row : row + 8]
                    im_part = raw[1, at, row : row + 8]
                    per_z.append(
                        (
                            re_part[:, :width] + im_part[:, width:],
                            im_part[:, :width] - re_part[:, width:],
                        )
                    )
                fields.append(per_z)
            plane_sq = aux_ref[0, row : row + 8, 0:1] + wx_ref[j : j + 1, :]
            weight = aux_ref[1, row : row + 8, 0:1]
            updated = []
            for q in range(full_z):
                c_real, c_imag = unit_sum(fields[0], q, -1)
                g_real, g_imag = unit_sum(fields[1], q, -1)
                signed = q - full_z if 2 * q >= full_z else q
                wave_sq = plane_sq + (2.0 * math.pi * signed / full_z) ** 2
                numerator = 1.0 + time_step * stabilizer * wave_sq
                denominator = numerator + time_step * kappa_grad * wave_sq * wave_sq
                inverse = weight / denominator
                keep = numerator * inverse
                mix = time_step * wave_sq * inverse
                updated.append((keep * c_real - mix * g_real, keep * c_imag - mix * g_imag))
            for z in range(full_z):
                real, imag = unit_sum(updated, z, 1)
                fil_ref[0, z, row : row + 8, :] = real
                fil_ref[1, z, row : row + 8, :] = imag
        rows = fil_ref[...].reshape(2 * full_z * padded, width)
        raw = triple(split(rows), weights, ((1,), (0,)))
        raw = raw.reshape(2, full_z, padded, 2 * width)
        real = raw[0, :, :, :width] - raw[1, :, :, width:]
        imag = raw[0, :, :, width:] + raw[1, :, :, :width]
        cos, sin = tw_cos[j : j + 1, :], tw_sin[j : j + 1, :]
        back_ref[j, 0] = real * cos - imag * sin
        back_ref[j, 1] = imag * cos + real * sin

    for z in range(full_z):
        section, plane = z // planes, z % planes
        for row in range(0, kk, 8):
            parts = [
                (back_ref[j, 0, z, row : row + 8, :], back_ref[j, 1, z, row : row + 8, :])
                for j in range(4)
            ]
            extra = None
            if has_extra and row == 0:
                extra = [
                    (back_ref[j, 0, z, kk : kk + 8, :], back_ref[j, 1, z, kk : kk + 8, :])
                    for j in range(4)
                ]
            for a in range(4):
                real, imag = unit_sum(parts, a, 1)
                if extra is not None:
                    extra_real, _ = unit_sum(extra, a, 1)
                    imag = imag * (1.0 - special) + extra_real * special
                for step in range(quarter):
                    target = section * slabs + a * quarter + step
                    piece = slice(step * lanes, (step + 1) * lanes)
                    at = plane * inner + row
                    out_ref[target, at : at + 8, :] = real[:, piece]
                    out_ref[target, at + kk : at + kk + 8, :] = imag[:, piece]
    if has_extra:
        for target in range(devices):
            out_ref[target, planes * inner :, :] = part_ref[...]


def kernel_call(body, out_shape, scratch, flops, moved, *operands):
    return pl.pallas_call(
        body,
        out_shape=jax.ShapeDtypeStruct(out_shape, jnp.float32),
        in_specs=[pl.BlockSpec(memory_space=pltpu.VMEM)] * len(operands),
        out_specs=pl.BlockSpec(memory_space=pltpu.VMEM),
        scratch_shapes=scratch,
        compiler_params=pltpu.CompilerParams(vmem_limit_bytes=vmem_limit),
        cost_estimate=pl.CostEstimate(flops=flops, bytes_accessed=moved, transcendentals=0),
    )(*operands)


def signed_square(index, length):
    signed = jnp.where(2 * index >= length, index - length, index)
    angle = signed.astype(jnp.float32) * (2.0 * math.pi / length)
    return angle * angle


def kernel_step(concentration):
    planes, rows, full_y = concentration.shape
    slabs = lax.axis_size("slab")
    sections = lax.axis_size("section")
    devices = slabs * sections
    full_x = rows * slabs
    full_z = planes * sections
    cells = full_x * full_y * full_z
    half = full_y // 2
    kk = half // 2 // devices
    width = full_x // 4
    me = lax.axis_index("section") * slabs + lax.axis_index("slab")
    axes = ("section", "slab")
    base = np.arange(width)
    step = 2.0 * math.pi / width
    coarse = base[::row_group, None] * base[None, :] % width * step
    fine = base[:row_group, None] * base[None, :] % width * step
    dft = [f(t).astype(np.float32) for t in (coarse, fine) for f in (np.cos, np.sin)]
    twist = np.arange(4)[:, None] * base[None, :] * (2.0 * math.pi / full_x)
    twist_cos, twist_sin = np.cos(twist).astype(np.float32), np.sin(twist).astype(np.float32)
    kx = np.arange(4)[:, None] + 4 * base[None, :]
    kx = np.where(2 * kx >= full_x, kx - full_x, kx) * (2.0 * math.pi / full_x)
    wave_x = (kx * kx).astype(np.float32)
    tables = [y_tables(full_y, devices, parity) for parity in range(2)]
    columns = planes * 2 * rows
    flops = 6 * half * half * columns
    squared = concentration * concentration
    bulk_sum = jnp.sum(0.25 * squared * squared - 0.5 * squared)
    arrived = []
    for parity in range(2):
        sent = kernel_call(
            functools.partial(forward_kernel, parity),
            (devices, 2 * kk, columns),
            [pltpu.VMEM((columns, half), jnp.bfloat16)] * 2,
            flops,
            4 * concentration.size + 4 * half * columns,
            concentration,
            *tables[parity],
        )
        arrived.append(lax.all_to_all(sent, axes, split_axis=0, concat_axis=0, tiled=True))
    returned = []
    for parity in range(2):
        has_extra = parity == 0
        padded = kk + 8 if has_extra else kk
        row = jnp.arange(padded, dtype=jnp.int32)
        wave = parity + 2 * (me * kk + row)
        extra_row = row >= kk
        if has_extra:
            wave = jnp.where(extra_row, half, wave)
        first = (wave == 0) | extra_row
        weight = jnp.where(first, 1.0 / cells, 2.0 / cells)
        flag = jnp.where((row == 0) & (me == 0), 1.0, 0.0)
        aux = jnp.stack([signed_square(wave, full_y), weight, flag]).astype(jnp.float32)
        aux = jnp.broadcast_to(aux[:, :, None], (3, padded, lanes))
        sent = kernel_call(
            functools.partial(middle_kernel, has_extra, sections),
            (devices, 2 * kk * planes + (8 if has_extra else 0), rows),
            [
                pltpu.VMEM((4, 2, 2 * full_z, padded, width), jnp.float32),
                pltpu.VMEM((2, full_z, padded, width), jnp.float32),
                pltpu.VMEM((4, 2, full_z, padded, width), jnp.float32),
            ],
            6 * 24 * full_z * padded * width * 2 * width,
            4 * half * columns,
            arrived[parity],
            aux,
            wave_x,
            twist_cos,
            twist_sin,
            *dft,
            *([jnp.full((8, lanes), bulk_sum)] if has_extra else []),
        )
        returned.append(lax.all_to_all(sent, axes, split_axis=0, concat_axis=0, tiled=True))
    even = kernel_call(
        backward_even_kernel,
        (planes * rows, half),
        [],
        flops // 2,
        8 * half * columns,
        returned[0],
        *tables[0],
    )
    new_field = kernel_call(
        backward_odd_kernel,
        concentration.shape,
        [],
        flops // 2,
        8 * half * columns,
        returned[1],
        even,
        *tables[1],
    )
    energy = jnp.sum(returned[0][:, 2 * kk * planes, 0]) / cells
    return (new_field, energy)


def per_device(concentration):
    planes, rows, full_y = concentration.shape
    devices = lax.axis_size("slab") * lax.axis_size("section")
    share = full_y // 4 // devices
    fits = (
        rows == lanes
        and planes * lax.axis_size("section") == 4
        and 2 * share == row_group
        and devices % 8 == 0
        and lax.axis_size("slab") % 4 == 0
    )
    return kernel_step(concentration) if fits else plain_step(concentration)


def solution(mesh):
    return jax.shard_map(
        per_device,
        mesh=mesh,
        in_specs=(P("section", "slab", None),),
        out_specs=(P("section", "slab", None), P()),
        check_vma=False,
    )
```

profile of v0, /device:TPU:0, one launch (start us, length us, event | category | flops | bytes accessed | tf_op | source)
XLA Modules:
  0.0 188.1 jit_solution(10721183070812238000)
XLA Ops:
  0.6 6.8 %shard_map.169 = f32[32,32,512]{2,1,0:T(8,128)} custom-call(f32[2,128,2048]{2,1,0:T(8,128)} %conc_ref.3, f32[32,1024]{1,0:T(8,128)} %constant.75.clone.ta, f32[32,1024]{1,0:T(8,128)} %constant.76.clone.tb, f32[32,1024]{1,0:T(8,128)} %constant.77.clone.tc, f32[32,1024]{1,0:T(8,128)} %constant.78.clone.td), custom_call_target="tpu_custom_call" | custom-call | flops 3221225472 | bytes 4194304 | tf_op jit(solution)/shard_map/pallas_call | solution.py:421
  7.5 7.5 %all-to-all-start.2 = ((f32[32,32,512]{2,1,0:T(8,128)}), f32[32,32,512]{2,1,0:T(8,128)}, u32[]{:S(2)}, u32[]{:S(2)}) async-start(f32[32,32,512]{2,1,0:T(8,128)} %shard_map.169), calls=%async_computation.2 | async-start | bytes 4194304 | tf_op jit(solution)/shard_map/all_to_all | solution.py:477
  14.9 6.8 %shard_map.167 = f32[32,32,512]{2,1,0:T(8,128)} custom-call(f32[2,128,2048]{2,1,0:T(8,128)} %conc_ref.3, f32[32,1024]{1,0:T(8,128)} %constant.79.clone.ta, f32[32,1024]{1,0:T(8,128)} %constant.80.clone.tb, f32[32,1024]{1,0:T(8,128)} %constant.77.clone.tc, f32[32,1024]{1,0:T(8,128)} %constant.78.clone.td), custom_call_target="tpu_custom_call" | custom-call | flops 3221225472 | bytes 4194304 | tf_op jit(solution)/shard_map/pallas_call | solution.py:421
  21.7 0.0 copy-start
  21.8 43.2 %all-to-all-done.2.in_ref = f32[32,32,512]{2,1,0:T(8,128)} async-done(((f32[32,32,512]{2,1,0:T(8,128)}), f32[32,32,512]{2,1,0:T(8,128)}, u32[]{:S(2)}, u32[]{:S(2)}) %all-to-all-start.2) | async-done | bytes 2097184 | tf_op jit(solution)/shard_map/all_to_all | solution.py:477
  65.0 3.7 %all-to-all-start = ((f32[32,32,512]{2,1,0:T(8,128)}), f32[32,32,512]{2,1,0:T(8,128)}, u32[]{:S(2)}, u32[]{:S(2)}) async-start(f32[32,32,512]{2,1,0:T(8,128)} %shard_map.167), calls=%async_computation | async-start | bytes 4194304 | tf_op jit(solution)/shard_map/all_to_all | solution.py:477
  68.7 0.0 copy-done
  68.7 1.1 fusion.1
  69.8 1.2 broadcast_in_dim.58.rest_0_
  71.1 0.7 broadcast_in_dim.57.aux_ref
  71.8 11.9 %shard_map.170 = f32[32,72,128]{2,1,0:T(8,128)} custom-call(f32[32,32,512]{2,1,0:T(8,128)} %all-to-all-done.2.in_ref, f32[3,24,128]{2,1,0:T(8,128)} %broadcast_in_dim.57.aux_ref, f32[4,512]{1,0:T(4,128)} %constant.81.clone.wx_ref, f32[4,512]{1,0:T(4,128)} %constant.82.clone.tw_cos, f32[4,512]{1,0:T(4,128)} %constant.83.clone.tw_sin, ...), custom_call_target="tpu_custom_call" | custom-call | flops 7247757312 | bytes 2097152 | tf_op jit(solution)/shard_map/pallas_call | solution.py:421
  83.6 34.9 %all-to-all-done.in_ref = f32[32,32,512]{2,1,0:T(8,128)} async-done(((f32[32,32,512]{2,1,0:T(8,128)}), f32[32,32,512]{2,1,0:T(8,128)}, u32[]{:S(2)}, u32[]{:S(2)}) %all-to-all-start) | async-done | bytes 2097184 | tf_op jit(solution)/shard_map/all_to_all | solution.py:477
  118.5 2.9 %all-to-all-start.3 = ((f32[32,72,128]{2,1,0:T(8,128)}), f32[32,72,128]{2,1,0:T(8,128)S(1)}, u32[]{:S(2)}, u32[]{:S(2)}) async-start(f32[32,72,128]{2,1,0:T(8,128)} %shard_map.170), calls=%async_computation.3 | async-start | bytes 2359296 | tf_op jit(solution)/shard_map/all_to_all | solution.py:510
  121.5 0.7 broadcast_in_dim.51.aux_ref
  122.2 9.4 %shard_map.168 = f32[32,64,128]{2,1,0:T(8,128)} custom-call(f32[32,32,512]{2,1,0:T(8,128)} %all-to-all-done.in_ref, f32[3,16,128]{2,1,0:T(8,128)} %broadcast_in_dim.51.aux_ref, f32[4,512]{1,0:T(4,128)} %constant.81.clone.wx_ref, f32[4,512]{1,0:T(4,128)} %constant.82.clone.tw_cos, f32[4,512]{1,0:T(4,128)} %constant.83.clone.tw_sin, ...), custom_call_target="tpu_custom_call" | custom-call | flops 4831838208 | bytes 2097152 | tf_op jit(solution)/shard_map/pallas_call | solution.py:421
  131.5 19.6 %all-to-all-done.3.in_ref = f32[32,72,128]{2,1,0:T(8,128)S(1)} async-done(((f32[32,72,128]{2,1,0:T(8,128)}), f32[32,72,128]{2,1,0:T(8,128)S(1)}, u32[]{:S(2)}, u32[]{:S(2)}) %all-to-all-start.3) | async-done | bytes 1179680 | tf_op jit(solution)/shard_map/all_to_all | solution.py:510
  151.2 0.0 copy-start.1
  151.2 2.6 %all-to-all-start.1 = ((f32[32,64,128]{2,1,0:T(8,128)}), f32[32,64,128]{2,1,0:T(8,128)S(1)}, u32[]{:S(2)}, u32[]{:S(2)}) async-start(f32[32,64,128]{2,1,0:T(8,128)} %shard_map.168), calls=%async_computation.1 | async-start | bytes 2097152 | tf_op jit(solution)/shard_map/all_to_all | solution.py:510
  153.8 0.6 slice_reduce_fusion
  155.1 0.0 copy-done.1
  155.1 4.4 %shard_map.171.even_ref = f32[256,1024]{1,0:T(8,128)} custom-call(f32[32,72,128]{2,1,0:T(8,128)} %copy-done.1, f32[32,1024]{1,0:T(8,128)} %constant.75.clone.ta, f32[32,1024]{1,0:T(8,128)} %constant.76.clone.tb, f32[32,1024]{1,0:T(8,128)} %constant.77.clone.tc, f32[32,1024]{1,0:T(8,128)} %constant.78.clone.td), custom_call_target="tpu_custom_call" | custom-call | flops 1610612736 | bytes 4194304 | tf_op jit(solution)/shard_map/pallas_call | solution.py:421
  159.5 21.5 %all-to-all-done.1.in_ref = f32[32,64,128]{2,1,0:T(8,128)S(1)} async-done(((f32[32,64,128]{2,1,0:T(8,128)}), f32[32,64,128]{2,1,0:T(8,128)S(1)}, u32[]{:S(2)}, u32[]{:S(2)}) %all-to-all-start.1) | async-done | bytes 1048608 | tf_op jit(solution)/shard_map/all_to_all | solution.py:510
  181.0 0.0 copy-start.2
  181.0 1.0 copy-done.2
  182.0 5.0 %shard_map.172 = f32[2,128,2048]{2,1,0:T(8,128)} custom-call(f32[32,64,128]{2,1,0:T(8,128)} %copy-done.2, f32[256,1024]{1,0:T(8,128)} %shard_map.171.even_ref, f32[32,1024]{1,0:T(8,128)} %constant.79.clone.ta, f32[32,1024]{1,0:T(8,128)} %constant.80.clone.tb, f32[32,1024]{1,0:T(8,128)} %constant.77.clone.tc, f32[32,1024]{1,0:T(8,128)} %constant.78.clone.td), custom_call_target="tpu_custom_call" | custom-call | flops 1610612736 | bytes 4194304 | tf_op jit(solution)/shard_map/pallas_call | solution.py:421
  (6 shorter events, 0.1 us)
Async XLA Ops:
  7.5 57.5 %all-to-all-start.2 = ((f32[32,32,512]{2,1,0:T(8,128)}), f32[32,32,512]{2,1,0:T(8,128)}, u32[]{:S(2)}, u32[]{:S(2)}) async-start(f32[32,32,512]{2,1,0:T(8,128)} %shard_map.169), calls=%async_computation.2 | async-start | bytes 4194304 | tf_op jit(solution)/shard_map/all_to_all | solution.py:477
  21.7 46.9 %copy-start = (f32[2,128,2048]{2,1,0:T(8,128)S(1)}, f32[2,128,2048]{2,1,0:T(8,128)}, u32[]{:S(2)}) copy-start(f32[2,128,2048]{2,1,0:T(8,128)} %conc_ref.3) | copy-start | bytes 6291460
  65.0 53.6 %all-to-all-start = ((f32[32,32,512]{2,1,0:T(8,128)}), f32[32,32,512]{2,1,0:T(8,128)}, u32[]{:S(2)}, u32[]{:S(2)}) async-start(f32[32,32,512]{2,1,0:T(8,128)} %shard_map.167), calls=%async_computation | async-start | bytes 4194304 | tf_op jit(solution)/shard_map/all_to_all | solution.py:477
  118.5 32.6 %all-to-all-start.3 = ((f32[32,72,128]{2,1,0:T(8,128)}), f32[32,72,128]{2,1,0:T(8,128)S(1)}, u32[]{:S(2)}, u32[]{:S(2)}) async-start(f32[32,72,128]{2,1,0:T(8,128)} %shard_map.170), calls=%async_computation.3 | async-start | bytes 2359296 | tf_op jit(solution)/shard_map/all_to_all | solution.py:510
  151.2 3.9 %copy-start.1 = (f32[32,72,128]{2,1,0:T(8,128)}, f32[32,72,128]{2,1,0:T(8,128)S(1)}, u32[]{:S(2)}) copy-start(f32[32,72,128]{2,1,0:T(8,128)S(1)} %all-to-all-done.3.in_ref) | copy-start | bytes 3538948
  151.2 29.8 %all-to-all-start.1 = ((f32[32,64,128]{2,1,0:T(8,128)}), f32[32,64,128]{2,1,0:T(8,128)S(1)}, u32[]{:S(2)}, u32[]{:S(2)}) async-start(f32[32,64,128]{2,1,0:T(8,128)} %shard_map.168), calls=%async_computation.1 | async-start | bytes 2097152 | tf_op jit(solution)/shard_map/all_to_all | solution.py:510
  181.0 1.0 copy-start.2
where the time goes:
time: 189 us; the launch traced here: 188 us
  waiting for transfers between devices  119 us (63%)
  Pallas kernels  44.3 us (23%)
  starting transfers between devices  16.6 us (9%)
  local copies, waits for them, and re-layouts  3.64 us (2%)
  between operations  2.51 us (1%)
    all_to_all x4, waiting for transfers between devices, kernel_step(): lax.all_to_all(sent, axes, split_axis=0, concat_axis=0, tiled=True)  119 us
    pallas_call x6, Pallas kernels, kernel_call(): pl.pallas_call(body, out_shape=jax.ShapeDtypeStruct(out_shape, jnp.float3...  44.3 us
    all_to_all x4, starting transfers between devices, kernel_step(): lax.all_to_all(sent, axes, split_axis=0, concat_axis=0, tiled=True)  16.6 us
  transfers between devices with their start and end apart: 4, of which 4 were waited for; matrix products, arithmetic and copies ran while one was open for 2% of the time, Pallas kernels for 17%

commit v1 on v0

v1 whole, which is shorter than its diff:
```python
import functools
import math

import jax
import jax.numpy as jnp
import numpy as np
from jax import lax
from jax.experimental import pallas as pl
from jax.experimental.pallas import tpu as pltpu
from jax.sharding import PartitionSpec as P

time_step = 100.0
kappa_grad = 2.0
stabilizer = 8.0
highest = lax.Precision.HIGHEST


def circle(length, first_total, second_total, direction):
    first_index = jnp.arange(first_total, dtype=jnp.int32)
    second_index = jnp.arange(second_total, dtype=jnp.int32)
    turn_index = first_index[:, None] * second_index[None, :] % length
    phase_angle = turn_index.astype(jnp.float32) * (2.0 * math.pi / length)
    return (jnp.cos(phase_angle), direction * jnp.sin(phase_angle))


def contract(pattern, real_part, imag_part, table_cos, table_sin):

    def product_of(operand, matrix):
        return jnp.einsum(pattern, operand, matrix, precision=highest)

    out_real = product_of(real_part, table_cos) - product_of(imag_part, table_sin)
    out_imag = product_of(real_part, table_sin) + product_of(imag_part, table_cos)
    return (out_real, out_imag)


def real_only(pattern, real_part, imag_part, table_cos, table_sin):
    return jnp.einsum(pattern, real_part, table_cos, precision=highest) - jnp.einsum(
        pattern, imag_part, table_sin, precision=highest
    )


def rotate(real_part, imag_part, table_cos, table_sin):
    return (
        real_part * table_cos - imag_part * table_sin,
        real_part * table_sin + imag_part * table_cos,
    )


def wave_square(storage, length, permuted):
    if permuted:
        actual = storage // 128 + length // 128 * (storage % 128)
    else:
        actual = storage
    signed = jnp.where(2 * actual >= length, actual - length, actual)
    phase_angle = signed.astype(jnp.float32) * (2.0 * math.pi / length)
    return phase_angle * phase_angle


def plain_step(concentration):
    plane_count, row_count, full_y = concentration.shape
    slab_count = lax.axis_size("slab")
    section_count = lax.axis_size("section")
    full_x = row_count * slab_count
    full_z = plane_count * section_count
    y_block = full_y // slab_count
    y_half = y_block // section_count
    blocks_x = full_x // 128
    blocks_y = full_y // 128
    cell_count = full_x * full_y * full_z
    slab_at = lax.axis_index("slab")
    section_at = lax.axis_index("section")
    squared = concentration * concentration
    bulk_sum = jnp.sum(0.25 * squared * squared - 0.5 * squared)
    cubic_term = squared * concentration - concentration
    shaped_c = concentration.reshape(1, plane_count, row_count, blocks_y, 128)
    shaped_g = cubic_term.reshape(1, plane_count, row_count, blocks_y, 128)
    first_cos, first_sin = circle(blocks_y, blocks_y, blocks_y, -1.0)
    part_real, part_imag = contract("fzxab,aj->fzxjb", shaped_c, shaped_g, first_cos, first_sin)
    field_total = part_real.shape[0]
    twist_cos, twist_sin = circle(full_y, blocks_y, 128, -1.0)
    part_real, part_imag = rotate(part_real, part_imag, twist_cos, twist_sin)
    lane_cos, lane_sin = circle(128, 128, 128, -1.0)
    part_real, part_imag = contract("fzxjb,bk->fxjkz", part_real, part_imag, lane_cos, lane_sin)
    outgoing = jnp.concatenate([part_real, part_imag], 0).reshape(
        2 * field_total, row_count, slab_count, y_block * plane_count
    )
    columns = lax.all_to_all(outgoing, "slab", split_axis=2, concat_axis=1, tiled=True)
    columns = columns.reshape(2 * field_total, blocks_x, 128, y_block * plane_count)
    first_cos, first_sin = circle(blocks_x, blocks_x, blocks_x, -1.0)
    part_real, part_imag = contract(
        "fabm,aj->fmjb", columns[:field_total], columns[field_total:], first_cos, first_sin
    )
    twist_cos, twist_sin = circle(full_x, blocks_x, 128, -1.0)
    part_real, part_imag = rotate(part_real, part_imag, twist_cos, twist_sin)
    part_real, part_imag = contract("fmjb,bk->fmjk", part_real, part_imag, lane_cos, lane_sin)
    spectra_x = jnp.concatenate([part_real, part_imag], 0).reshape(
        2 * field_total, y_block, plane_count, full_x
    )
    depth_cos, depth_sin = circle(full_z, full_z, full_z, -1.0)
    own_cos = lax.dynamic_slice_in_dim(depth_cos, section_at * plane_count, plane_count, 0)
    own_sin = lax.dynamic_slice_in_dim(depth_sin, section_at * plane_count, plane_count, 0)
    term_real, term_imag = contract(
        "fyzk,zq->yfqk", spectra_x[:field_total], spectra_x[field_total:], own_cos, own_sin
    )
    spectral = lax.psum_scatter(
        jnp.concatenate([term_real, term_imag], 1), "section", scatter_dimension=0, tiled=True
    )
    storage_y = slab_at * y_block + section_at * y_half + jnp.arange(y_half, dtype=jnp.int32)
    storage_x = jnp.arange(full_x, dtype=jnp.int32)
    storage_z = jnp.arange(full_z, dtype=jnp.int32)
    wave_sq = (
        wave_square(storage_y, full_y, True)[:, None, None]
        + wave_square(storage_z, full_z, False)[None, :, None]
        + wave_square(storage_x, full_x, True)[None, None, :]
    )
    numerator = 1.0 + time_step * stabilizer * wave_sq
    denominator = numerator + time_step * kappa_grad * wave_sq * wave_sq
    keep_rate = numerator / denominator
    mix_rate = time_step * wave_sq / denominator
    new_real = keep_rate * spectral[:, 0] - mix_rate * spectral[:, 1]
    new_imag = keep_rate * spectral[:, 1] + mix_rate * spectral[:, 0]
    back_cos, back_sin = circle(full_z, full_z, full_z, 1.0)
    part_real, part_imag = contract("yqk,qz->yzk", new_real, new_imag, back_cos, back_sin)
    returning = jnp.stack([part_real, part_imag], 1)
    own_planes = lax.all_to_all(returning, "section", split_axis=2, concat_axis=0, tiled=True)
    grid_real = own_planes[:, 0].reshape(y_block, plane_count, blocks_x, 128)
    grid_imag = own_planes[:, 1].reshape(y_block, plane_count, blocks_x, 128)
    lane_cos, lane_sin = circle(128, 128, 128, 1.0)
    part_real, part_imag = contract("szjk,kb->szjb", grid_real, grid_imag, lane_cos, lane_sin)
    twist_cos, twist_sin = circle(full_x, blocks_x, 128, 1.0)
    part_real, part_imag = rotate(part_real, part_imag, twist_cos, twist_sin)
    first_cos, first_sin = circle(blocks_x, blocks_x, blocks_x, 1.0)
    part_real, part_imag = contract("szjb,ja->absz", part_real, part_imag, first_cos, first_sin)
    leaving = jnp.stack([part_real, part_imag], 0).reshape(2, full_x, 1, y_block * plane_count)
    rows_back = lax.all_to_all(leaving, "slab", split_axis=1, concat_axis=2, tiled=True)
    rows_back = rows_back.reshape(2, row_count, blocks_y, 128, plane_count)
    part_real, part_imag = contract("xjkz,kb->xjbz", rows_back[0], rows_back[1], lane_cos, lane_sin)
    twist_cos, twist_sin = circle(full_y, blocks_y, 128, 1.0)
    part_real, part_imag = rotate(
        part_real, part_imag, twist_cos[:, :, None], twist_sin[:, :, None]
    )
    first_cos, first_sin = circle(blocks_y, blocks_y, blocks_y, 1.0)
    new_field = real_only("xjbz,ja->zxab", part_real, part_imag, first_cos, first_sin)
    new_field = new_field.reshape(plane_count, row_count, full_y) / cell_count
    total_bulk = lax.psum(bulk_sum, ("section", "slab"))
    energy = total_bulk / cell_count
    return (new_field, energy)


lanes = 128
row_group = 32
vmem_limit = 62 * 1024 * 1024


def split(values):
    high = values.astype(jnp.bfloat16)
    low = (values - high.astype(jnp.float32)).astype(jnp.bfloat16)
    return high, low


def triple(left_parts, right_parts, dims):
    def product(left, right):
        return lax.dot_general(left, right, (dims, ((), ())), preferred_element_type=jnp.float32)

    left_high, left_low = left_parts
    right_high, right_low = right_parts
    return (
        product(left_high, right_high)
        + product(left_low, right_high)
        + product(left_high, right_low)
    )


def y_tables(full_y, devices, parity):
    half = full_y // 2
    per_part = half // 2 // devices
    slot = np.arange(half)
    device, inner = slot // (2 * per_part), slot % (2 * per_part)
    part, local = inner // per_part, inner % per_part
    wave = parity + 2 * (device * per_part + local)
    position = np.arange(half)
    turns = wave[:, None] * position[None, :] % full_y
    phase = turns * (2.0 * math.pi / full_y)
    coarse = phase[::row_group]
    offset = wave[:row_group] - wave[0]
    fine = (offset[:, None] * position[None, :] % full_y) * (2.0 * math.pi / full_y)
    fine = fine + part[:row_group, None] * (0.5 * math.pi)
    return [
        table.astype(np.float32)
        for table in (np.cos(coarse), np.sin(coarse), np.cos(fine), np.sin(fine))
    ]


def y_block(refs, block, groups, parity):
    coarse_cos, coarse_sin, fine_cos, fine_sin = refs
    cos_fine, sin_fine = fine_cos[...], fine_sin[...]
    pieces = []
    for inner in range(groups):
        at = pl.ds(block * groups + inner, 1)
        piece = coarse_cos[at, :] * cos_fine - coarse_sin[at, :] * sin_fine
        if parity == 0 and inner == 0:
            row = lax.broadcasted_iota(jnp.int32, piece.shape, 0)
            column = lax.broadcasted_iota(jnp.int32, piece.shape, 1)
            sign = 1.0 - 2.0 * (column % 2).astype(jnp.float32)
            wanted = jnp.where(block == 0, row_group // 2, -1)
            piece = jnp.where(row == wanted, sign, piece)
        pieces.append(piece)
    return jnp.concatenate(pieces, 0)


def times_unit(real, imag, quarter_turns):
    turns = quarter_turns % 4
    if turns == 0:
        return real, imag
    if turns == 1:
        return -imag, real
    if turns == 2:
        return -real, -imag
    return imag, -real


def unit_sum(parts, power, direction):
    total_real, total_imag = parts[0]
    for index in range(1, len(parts)):
        real, imag = times_unit(*parts[index], direction * power * index)
        total_real = total_real + real
        total_imag = total_imag + imag
    return total_real, total_imag


groups = 8
chunks = 4


def flip(bit, wanted):
    return 1 - bit if wanted else bit


class Place:
    def __init__(self):
        self.section = lax.axis_index("section")
        self.slab = lax.axis_index("slab")
        self.upper = self.slab // 8
        self.bits = [self.slab % 2, self.slab // 2 % 2, self.slab // 4 % 2, self.section]
        self.member = self.index_of(self.bits)

    @staticmethod
    def index_of(bits):
        return bits[3] * 8 + bits[2] * 4 + bits[1] * 2 + bits[0]

    def peer(self, turn):
        bits = [flip(bit, turn >> at & 1) for at, bit in enumerate(self.bits)]
        slab = self.upper * 8 + bits[2] * 4 + bits[1] * 2 + bits[0]
        return self.index_of(bits), (bits[3], slab)

    def partner(self):
        return self.section, (1 - self.upper) * 8 + self.slab % 8


def remote(source, target, send, receive, device):
    return pltpu.make_async_remote_copy(
        src_ref=source,
        dst_ref=target,
        send_sem=send,
        recv_sem=receive,
        device_id=device,
        device_id_type=pl.DeviceIdType.MESH,
    )


turn_order = list(range(1, 16))


def greet(place):
    barrier = pltpu.get_barrier_semaphore()
    devices = [place.peer(turn)[1] for turn in turn_order] + [place.partner()]
    for device in devices:
        pl.semaphore_signal(
            barrier, inc=1, device_id=device, device_id_type=pl.DeviceIdType.MESH
        )
    pl.semaphore_wait(barrier, len(devices))


def step_kernel(cells, conc_ref, *refs):
    tables = [refs[0:4], refs[4:8]]
    wx_ref, tw_cos, tw_sin, ca, sa, cb, sb = refs[8:15]
    out_ref, energy_ref = refs[15:17]
    (
        high_ref, low_ref, wide_high, wide_low, spec_ref, fil_ref, back_ref, even_ref,
        sent_ref, arrived_ref, own_ref, other_ref, partner_ref, returned_ref,
        tile_ref, half_ref, far_ref,
        sent_out, sent_in, other_out, other_in, own_out, own_in, tile_out, tile_in,
        half_out, half_in,
    ) = refs[17:]
    place = Place()
    member = place.member
    planes, rows, full_y = conc_ref.shape
    half = full_y // 2
    members, inner, columns = arrived_ref.shape[1:]
    kk = inner // 2
    width = spec_ref.shape[4]
    padded = kk + 8
    sections = 2
    full_z = planes * sections
    zf_local = planes * 2
    total_zf = zf_local * sections
    slabs = members // sections
    quarter = slabs // 2
    greet(place)

    def prepare(parity):
        total = jnp.zeros((8, lanes), jnp.float32)
        for plane in range(planes):
            first = conc_ref[plane, :, :half]
            second = conc_ref[plane, :, half:]
            first_sq, second_sq = first * first, second * second
            if parity == 0:
                bulk = 0.25 * (first_sq * first_sq + second_sq * second_sq)
                bulk = bulk - 0.5 * (first_sq + second_sq)
                bulk = jnp.sum(bulk.reshape(rows // 8, 8, half), axis=0)
                for at in range(0, half, lanes):
                    total = total + bulk[:, at : at + lanes]
            first_g = first_sq * first - first
            second_g = second_sq * second - second
            for field, (left, right) in enumerate(((first, second), (first_g, second_g))):
                mixed = left + right if parity == 0 else left - right
                high, low = split(mixed)
                at = (plane * 2 + field) * rows
                high_ref[at : at + rows, :] = high
                low_ref[at : at + rows, :] = low
        return total

    def forward(chunk):
        parity, sub = chunk // 2, chunk % 2
        blocks = members // groups

        def one(block, carry):
            table = y_block(tables[parity], sub * blocks + block, groups, parity)
            result = triple(split(table), (high_ref[...], low_ref[...]), ((1,), (1,)))
            sent_ref[chunk, pl.ds(block * groups, groups)] = result.reshape(groups, inner, columns)
            return carry

        lax.fori_loop(0, blocks, one, 0)
        arrived_ref[chunk, member] = sent_ref[chunk, member]

    def spread(chunk):
        copies = []
        for turn in turn_order:
            peer, device = place.peer(turn)
            copies.append(
                remote(
                    sent_ref.at[chunk, peer],
                    arrived_ref.at[chunk, member],
                    sent_out.at[chunk, turn],
                    sent_in.at[chunk, turn],
                    device,
                )
            )
        for copy in copies:
            copy.start()
        return copies

    def spread_tile():
        copies = []
        for turn in turn_order:
            copies.append(
                remote(
                    tile_ref.at[member],
                    tile_ref.at[member],
                    tile_out.at[turn],
                    tile_in.at[turn],
                    place.peer(turn)[1],
                )
            )
        for copy in copies:
            copy.start()
        return copies

    def middle(chunk):
        parity, sub = chunk // 2, chunk % 2
        has_extra = chunk == 0
        depth = padded if has_extra else kk
        base_wave = parity + 2 * kk * (sub * members + member)
        row_iota = lax.broadcasted_iota(jnp.int32, (8, 1), 0)
        special = None
        if has_extra:
            wanted = jnp.where(member == 0, 0, -1)
            special = jnp.where(row_iota == wanted, 1.0, 0.0)

        def gather(section, a, part, row, zf):
            pieces = [
                arrived_ref[
                    chunk,
                    section * slabs + a * quarter + step,
                    part * kk + row : part * kk + row + 8,
                    zf * lanes : (zf + 1) * lanes,
                ]
                for step in range(quarter)
            ]
            return jnp.concatenate(pieces, 1)

        for section in range(sections):
            for zf in range(zf_local):
                at = section * zf_local + zf
                for row in range(0, depth, 8):
                    source = 0 if row >= kk else row
                    parts = []
                    for a in range(2):
                        imag = gather(section, a, 1, source, zf)
                        if row >= kk:
                            real, imag = imag * special, jnp.zeros_like(imag)
                        else:
                            real = gather(section, a, 0, source, zf)
                            if has_extra and row == 0:
                                imag = imag * (1.0 - special)
                        parts.append((real, imag))
                    for j in range(4):
                        real, imag = unit_sum(parts, j, -1)
                        if j:
                            cos, sin = tw_cos[j : j + 1, :], tw_sin[j : j + 1, :]
                            real, imag = real * cos + imag * sin, imag * cos - real * sin
                        spec_ref[j, 0, at, row : row + 8, :] = real
                        spec_ref[j, 1, at, row : row + 8, :] = imag

        def one(j, carry):
            source = spec_ref[j, :, :, 0:depth, :].reshape(2 * total_zf * depth, width)
            weights = (wide_high[...], wide_low[...])
            raw = triple(split(source), weights, ((1,), (0,)))
            raw = raw.reshape(2, total_zf, depth, 2 * width)
            for row in range(0, depth, 8):
                fields = []
                for field in range(2):
                    per_z = []
                    for z in range(full_z):
                        at = z * 2 + field
                        re_part = raw[0, at, row : row + 8]
                        im_part = raw[1, at, row : row + 8]
                        per_z.append(
                            (
                                re_part[:, :width] + im_part[:, width:],
                                im_part[:, :width] - re_part[:, width:],
                            )
                        )
                    fields.append(per_z)
                wave = base_wave + 2 * (row + row_iota)
                if row >= kk:
                    wave = jnp.full_like(wave, half)
                first = (wave == 0) | (wave == half)
                weight = jnp.where(first, 1.0 / cells, 2.0 / cells)
                angle = wave.astype(jnp.float32) * (2.0 * math.pi / full_y)
                plane_sq = angle * angle + wx_ref[pl.ds(j, 1), :]
                updated = []
                for q in range(full_z):
                    c_real, c_imag = unit_sum(fields[0], q, -1)
                    g_real, g_imag = unit_sum(fields[1], q, -1)
                    signed = q - full_z if 2 * q >= full_z else q
                    wave_sq = plane_sq + (2.0 * math.pi * signed / full_z) ** 2
                    numerator = 1.0 + time_step * stabilizer * wave_sq
                    denominator = numerator + time_step * kappa_grad * wave_sq * wave_sq
                    inverse = weight / denominator
                    keep = numerator * inverse
                    mix = time_step * wave_sq * inverse
                    updated.append((keep * c_real - mix * g_real, keep * c_imag - mix * g_imag))
                for z in range(full_z):
                    real, imag = unit_sum(updated, z, 1)
                    fil_ref[0, z, row : row + 8, :] = real
                    fil_ref[1, z, row : row + 8, :] = imag
            source = fil_ref[:, :, 0:depth, :].reshape(2 * full_z * depth, width)
            raw = triple(split(source), weights, ((1,), (0,)))
            raw = raw.reshape(2, full_z, depth, 2 * width)
            real = raw[0, :, :, :width] - raw[1, :, :, width:]
            imag = raw[0, :, :, width:] + raw[1, :, :, :width]
            cos, sin = tw_cos[pl.ds(j, 1), :], tw_sin[pl.ds(j, 1), :]
            back_ref[j, 0, :, 0:depth, :] = real * cos - imag * sin
            back_ref[j, 1, :, 0:depth, :] = imag * cos + real * sin
            return carry

        lax.fori_loop(0, 4, one, 0)
        for z in range(full_z):
            section, plane = z // planes, z % planes
            for row in range(0, kk, 8):
                parts = [
                    (back_ref[j, 0, z, row : row + 8, :], back_ref[j, 1, z, row : row + 8, :])
                    for j in range(4)
                ]
                extra = None
                if has_extra and row == 0:
                    extra = [
                        (back_ref[j, 0, z, kk : kk + 8, :], back_ref[j, 1, z, kk : kk + 8, :])
                        for j in range(4)
                    ]
                for a in range(4):
                    real, imag = unit_sum(parts, a, 1)
                    if extra is not None:
                        extra_real, _ = unit_sum(extra, a, 1)
                        imag = imag * (1.0 - special) + extra_real * special
                    target_ref = own_ref if a < 2 else other_ref
                    for step in range(quarter):
                        target = section * slabs + a % 2 * quarter + step
                        piece = slice(step * lanes, (step + 1) * lanes)
                        at = plane * inner + row
                        target_ref[chunk, target, at : at + 8, :] = real[:, piece]
                        target_ref[chunk, target, at + kk : at + kk + 8, :] = imag[:, piece]

    def cross(chunk):
        copy = remote(
            other_ref.at[chunk],
            partner_ref.at[chunk],
            other_out.at[chunk],
            other_in.at[chunk],
            place.partner(),
        )
        copy.start()
        return copy

    def join(chunk):
        own_ref[chunk] = own_ref[chunk] + partner_ref[chunk]
        returned_ref[chunk, member] = own_ref[chunk, member]

    def give_back(chunk):
        copies = []
        for turn in turn_order:
            peer, device = place.peer(turn)
            copies.append(
                remote(
                    own_ref.at[chunk, peer],
                    returned_ref.at[chunk, member],
                    own_out.at[chunk, turn],
                    own_in.at[chunk, turn],
                    device,
                )
            )
        for copy in copies:
            copy.start()
        return copies

    def backward(chunk):
        parity, sub = chunk // 2, chunk % 2
        blocks = members // groups
        total = None
        for block in range(blocks):
            at = slice(block * groups, (block + 1) * groups)
            turned = [
                returned_ref[chunk, at, plane * inner : (plane + 1) * inner, :]
                .reshape(groups * inner, rows)
                .T
                for plane in range(planes)
            ]
            table = y_block(tables[parity], sub * blocks + block, groups, parity)
            term = triple(split(jnp.concatenate(turned, 0)), split(table), ((1,), (0,)))
            total = term if total is None else total + term
        return total

    def wait_in(copies):
        for copy in copies:
            copy.wait_recv()

    tile_ref[member] = prepare(0)
    forward(0)
    spreads = {0: spread(0)}
    tiles = spread_tile()
    forward(1)
    spreads[1] = spread(1)
    cos_rows, sin_rows = [], []
    cos_fine, sin_fine = cb[...], sb[...]
    for group in range(ca.shape[0]):
        cos_base, sin_base = ca[group : group + 1, :], sa[group : group + 1, :]
        cos_rows.append(cos_base * cos_fine - sin_base * sin_fine)
        sin_rows.append(sin_base * cos_fine + cos_base * sin_fine)
    table = jnp.concatenate([jnp.concatenate(cos_rows, 0), jnp.concatenate(sin_rows, 0)], 1)
    wide_high[...], wide_low[...] = split(table)
    prepare(1)
    forward(2)
    forward(3)
    crosses = {}
    backs = {}
    wait_in(spreads[0])
    middle(0)
    crosses[0] = cross(0)
    spreads[2] = spread(2)
    wait_in(tiles)
    half_ref[...] = jnp.sum(tile_ref[...], axis=0)
    far = remote(half_ref, far_ref, half_out, half_in, place.partner())
    far.start()
    wait_in(spreads[1])
    middle(1)
    crosses[1] = cross(1)
    spreads[3] = spread(3)
    wait_in(spreads[2])
    middle(2)
    crosses[2] = cross(2)
    crosses[0].wait_recv()
    join(0)
    backs[0] = give_back(0)
    wait_in(spreads[3])
    middle(3)
    crosses[3] = cross(3)
    crosses[1].wait_recv()
    join(1)
    backs[1] = give_back(1)
    crosses[2].wait_recv()
    join(2)
    backs[2] = give_back(2)
    wait_in(backs[0])
    even_ref[...] = backward(0)
    wait_in(backs[1])
    even_ref[...] = even_ref[...] + backward(1)
    crosses[3].wait_recv()
    join(3)
    backs[3] = give_back(3)
    wait_in(backs[2])
    odd = backward(2)
    wait_in(backs[3])
    odd = odd + backward(3)
    for plane in range(planes):
        even_rows = even_ref[plane * rows : (plane + 1) * rows, :]
        odd_rows = odd[plane * rows : (plane + 1) * rows, :]
        out_ref[plane, :, :half] = even_rows + odd_rows
        out_ref[plane, :, half:] = even_rows - odd_rows
    far.wait_recv()
    energy_ref[0, 0] = jnp.sum(half_ref[...] + far_ref[...]) / cells
    for chunk in range(chunks):
        for copy in spreads[chunk] + backs[chunk] + [crosses[chunk]]:
            copy.wait_send()
    for copy in tiles + [far]:
        copy.wait_send()


def kernel_step(concentration):
    planes, rows, full_y = concentration.shape
    slabs = lax.axis_size("slab")
    sections = lax.axis_size("section")
    devices = slabs * sections
    members = devices // 2
    full_x = rows * slabs
    full_z = planes * sections
    cells = full_x * full_y * full_z
    half = full_y // 2
    kk = half // 2 // devices
    width = full_x // 4
    base = np.arange(width)
    step = 2.0 * math.pi / width
    coarse = base[::row_group, None] * base[None, :] % width * step
    fine = base[:row_group, None] * base[None, :] % width * step
    dft = [f(t).astype(np.float32) for t in (coarse, fine) for f in (np.cos, np.sin)]
    twist = np.arange(4)[:, None] * base[None, :] * (2.0 * math.pi / full_x)
    twist_cos, twist_sin = np.cos(twist).astype(np.float32), np.sin(twist).astype(np.float32)
    kx = np.arange(4)[:, None] + 4 * base[None, :]
    kx = np.where(2 * kx >= full_x, kx - full_x, kx) * (2.0 * math.pi / full_x)
    wave_x = (kx * kx).astype(np.float32)
    tables = [y_tables(full_y, devices, parity) for parity in range(2)]
    columns = planes * 2 * rows
    operands = [concentration, *tables[0], *tables[1], wave_x, twist_cos, twist_sin, *dft]
    f32, bf16 = jnp.float32, jnp.bfloat16
    back_rows = 2 * kk * planes
    dma = pltpu.SemaphoreType.DMA
    new_field, energy = pl.pallas_call(
        functools.partial(step_kernel, cells),
        out_shape=(
            jax.ShapeDtypeStruct(concentration.shape, f32),
            jax.ShapeDtypeStruct((1, 1), f32),
        ),
        in_specs=[pl.BlockSpec(memory_space=pltpu.VMEM)] * len(operands),
        out_specs=(
            pl.BlockSpec(memory_space=pltpu.VMEM),
            pl.BlockSpec(memory_space=pltpu.SMEM),
        ),
        scratch_shapes=[
            pltpu.VMEM((columns, half), bf16),
            pltpu.VMEM((columns, half), bf16),
            pltpu.VMEM((width, 2 * width), bf16),
            pltpu.VMEM((width, 2 * width), bf16),
            pltpu.VMEM((4, 2, 2 * full_z, kk + 8, width), f32),
            pltpu.VMEM((2, full_z, kk + 8, width), f32),
            pltpu.VMEM((4, 2, full_z, kk + 8, width), f32),
            pltpu.VMEM((planes * rows, half), f32),
            pltpu.VMEM((chunks, members, 2 * kk, columns), f32),
            pltpu.VMEM((chunks, members, 2 * kk, columns), f32),
            pltpu.VMEM((chunks, members, back_rows, rows), f32),
            pltpu.VMEM((chunks, members, back_rows, rows), f32),
            pltpu.VMEM((chunks, members, back_rows, rows), f32),
            pltpu.VMEM((chunks, members, back_rows, rows), f32),
            pltpu.VMEM((members, 8, lanes), f32),
            pltpu.VMEM((8, lanes), f32),
            pltpu.VMEM((8, lanes), f32),
            dma((chunks, members)),
            dma((chunks, members)),
            dma((chunks,)),
            dma((chunks,)),
            dma((chunks, members)),
            dma((chunks, members)),
            dma((members,)),
            dma((members,)),
            dma,
            dma,
        ],
        compiler_params=pltpu.CompilerParams(
            vmem_limit_bytes=vmem_limit, collective_id=0, has_side_effects=True
        ),
    )(*operands)
    return (new_field, energy.reshape(()))


def per_device(concentration):
    planes, rows, full_y = concentration.shape
    devices = lax.axis_size("slab") * lax.axis_size("section")
    share = full_y // 4 // devices
    fits = (
        rows == lanes
        and planes * lax.axis_size("section") == 4
        and 2 * share == row_group
        and devices == 32
        and lax.axis_size("section") == 2
    )
    return kernel_step(concentration) if fits else plain_step(concentration)


def solution(mesh):
    return jax.shard_map(
        per_device,
        mesh=mesh,
        in_specs=(P("section", "slab", None),),
        out_specs=(P("section", "slab", None), P()),
        check_vma=False,
    )
```

time: 189 us -> 147 us (0.78)
  waiting for transfers between devices: 119 us -> 0 us
  Pallas kernels: 44.3 us -> 142 us
  starting transfers between devices: 16.6 us -> 0 us
    all_to_all x4 -> x0, waiting for transfers between devices: 119 us -> none  [kernel_step(): lax.all_to_all(sent, axes, split_axis=0, concat_axis=0, tiled=True)]
    pallas_call x6 -> x1, Pallas kernels: 44.3 us -> 142 us  [kernel_step(): pl.pallas_call(functools.partial(step_kernel, cells), out_shape=(jax.Shap...]
    all_to_all x4 -> x0, starting transfers between devices: 16.6 us -> none  [kernel_step(): lax.all_to_all(sent, axes, split_axis=0, concat_axis=0, tiled=True)]
    broadcast_in_dim x3 -> x0, local copies, waits for them, and re-layouts: 2.6 us -> none  [the longest x2 1.36 us: kernel_step(): aux = jnp.broadcast_to(aux[:, :, None], (3, padded, lanes))]
    unnamed x6 -> x1, local copies, waits for them, and re-layouts: 1.04 us -> 3.14 us
  transfers between devices with their start and end apart: 4 -> 0, of which waited for: 4 -> 0; matrix products, arithmetic and copies ran while one was open for 2% -> 0% of each run, Pallas kernels for 17% -> 0%
where the time goes in v1:
time: 147 us
  Pallas kernels  142 us (97%)
  local copies, waits for them, and re-layouts  3.14 us (2%)
  between operations  2.37 us (2%)
    pallas_call x1, Pallas kernels, kernel_step(): pl.pallas_call(functools.partial(step_kernel, cells), out_shape=(jax.Shap...  142 us
    unnamed x1, local copies, waits for them, and re-layouts  3.14 us

profile of v1, /device:TPU:0, one launch (start us, length us, event | category | flops | bytes accessed | tf_op | source)
XLA Modules:
  0.0 147.2 jit_solution(564400350808116613)
XLA Ops:
  0.6 141.7 %shard_map.167 = (f32[2,128,2048]{2,1,0:T(8,128)}, f32[1,1]{1,0:T(1,128)}) custom-call(f32[2,128,2048]{2,1,0:T(8,128)} %conc_ref.1, f32[32,1024]{1,0:T(8,128)} %constant.26.clone.refs_0_, f32[32,1024]{1,0:T(8,128)} %constant.27.clone.refs_1_, f32[32,1024]{1,0:T(8,128)} %constant.28.clone.refs_2_.refs_6_, f32[32,1024]{1,0:T(8,128)} %constant.29.clone.refs_3_.refs_7_, ...), custom_call_target="tpu_custom_call" | custom-call | tf_op jit(solution)/shard_map/pallas_call | solution.py:657
  142.3 3.1 %copy.20 = f32[2,128,2048]{2,1,0:T(8,128)} copy(f32[2,128,2048]{2,1,0:T(8,128)} %get-tuple-element.8) | data formatting | bytes 4194304

commit v2 on v1

v2 whole, which is shorter than its diff:
```python
import functools
import math

import jax
import jax.numpy as jnp
import numpy as np
from jax import lax
from jax.experimental import pallas as pl
from jax.experimental.pallas import tpu as pltpu
from jax.sharding import PartitionSpec as P

time_step = 100.0
kappa_grad = 2.0
stabilizer = 8.0
highest = lax.Precision.HIGHEST


def circle(length, first_total, second_total, direction):
    first_index = jnp.arange(first_total, dtype=jnp.int32)
    second_index = jnp.arange(second_total, dtype=jnp.int32)
    turn_index = first_index[:, None] * second_index[None, :] % length
    phase_angle = turn_index.astype(jnp.float32) * (2.0 * math.pi / length)
    return (jnp.cos(phase_angle), direction * jnp.sin(phase_angle))


def contract(pattern, real_part, imag_part, table_cos, table_sin):

    def product_of(operand, matrix):
        return jnp.einsum(pattern, operand, matrix, precision=highest)

    out_real = product_of(real_part, table_cos) - product_of(imag_part, table_sin)
    out_imag = product_of(real_part, table_sin) + product_of(imag_part, table_cos)
    return (out_real, out_imag)


def real_only(pattern, real_part, imag_part, table_cos, table_sin):
    return jnp.einsum(pattern, real_part, table_cos, precision=highest) - jnp.einsum(
        pattern, imag_part, table_sin, precision=highest
    )


def rotate(real_part, imag_part, table_cos, table_sin):
    return (
        real_part * table_cos - imag_part * table_sin,
        real_part * table_sin + imag_part * table_cos,
    )


def wave_square(storage, length, permuted):
    if permuted:
        actual = storage // 128 + length // 128 * (storage % 128)
    else:
        actual = storage
    signed = jnp.where(2 * actual >= length, actual - length, actual)
    phase_angle = signed.astype(jnp.float32) * (2.0 * math.pi / length)
    return phase_angle * phase_angle


def plain_step(concentration):
    plane_count, row_count, full_y = concentration.shape
    slab_count = lax.axis_size("slab")
    section_count = lax.axis_size("section")
    full_x = row_count * slab_count
    full_z = plane_count * section_count
    y_block = full_y // slab_count
    y_half = y_block // section_count
    blocks_x = full_x // 128
    blocks_y = full_y // 128
    cell_count = full_x * full_y * full_z
    slab_at = lax.axis_index("slab")
    section_at = lax.axis_index("section")
    squared = concentration * concentration
    bulk_sum = jnp.sum(0.25 * squared * squared - 0.5 * squared)
    cubic_term = squared * concentration - concentration
    shaped_c = concentration.reshape(1, plane_count, row_count, blocks_y, 128)
    shaped_g = cubic_term.reshape(1, plane_count, row_count, blocks_y, 128)
    first_cos, first_sin = circle(blocks_y, blocks_y, blocks_y, -1.0)
    part_real, part_imag = contract("fzxab,aj->fzxjb", shaped_c, shaped_g, first_cos, first_sin)
    field_total = part_real.shape[0]
    twist_cos, twist_sin = circle(full_y, blocks_y, 128, -1.0)
    part_real, part_imag = rotate(part_real, part_imag, twist_cos, twist_sin)
    lane_cos, lane_sin = circle(128, 128, 128, -1.0)
    part_real, part_imag = contract("fzxjb,bk->fxjkz", part_real, part_imag, lane_cos, lane_sin)
    outgoing = jnp.concatenate([part_real, part_imag], 0).reshape(
        2 * field_total, row_count, slab_count, y_block * plane_count
    )
    columns = lax.all_to_all(outgoing, "slab", split_axis=2, concat_axis=1, tiled=True)
    columns = columns.reshape(2 * field_total, blocks_x, 128, y_block * plane_count)
    first_cos, first_sin = circle(blocks_x, blocks_x, blocks_x, -1.0)
    part_real, part_imag = contract(
        "fabm,aj->fmjb", columns[:field_total], columns[field_total:], first_cos, first_sin
    )
    twist_cos, twist_sin = circle(full_x, blocks_x, 128, -1.0)
    part_real, part_imag = rotate(part_real, part_imag, twist_cos, twist_sin)
    part_real, part_imag = contract("fmjb,bk->fmjk", part_real, part_imag, lane_cos, lane_sin)
    spectra_x = jnp.concatenate([part_real, part_imag], 0).reshape(
        2 * field_total, y_block, plane_count, full_x
    )
    depth_cos, depth_sin = circle(full_z, full_z, full_z, -1.0)
    own_cos = lax.dynamic_slice_in_dim(depth_cos, section_at * plane_count, plane_count, 0)
    own_sin = lax.dynamic_slice_in_dim(depth_sin, section_at * plane_count, plane_count, 0)
    term_real, term_imag = contract(
        "fyzk,zq->yfqk", spectra_x[:field_total], spectra_x[field_total:], own_cos, own_sin
    )
    spectral = lax.psum_scatter(
        jnp.concatenate([term_real, term_imag], 1), "section", scatter_dimension=0, tiled=True
    )
    storage_y = slab_at * y_block + section_at * y_half + jnp.arange(y_half, dtype=jnp.int32)
    storage_x = jnp.arange(full_x, dtype=jnp.int32)
    storage_z = jnp.arange(full_z, dtype=jnp.int32)
    wave_sq = (
        wave_square(storage_y, full_y, True)[:, None, None]
        + wave_square(storage_z, full_z, False)[None, :, None]
        + wave_square(storage_x, full_x, True)[None, None, :]
    )
    numerator = 1.0 + time_step * stabilizer * wave_sq
    denominator = numerator + time_step * kappa_grad * wave_sq * wave_sq
    keep_rate = numerator / denominator
    mix_rate = time_step * wave_sq / denominator
    new_real = keep_rate * spectral[:, 0] - mix_rate * spectral[:, 1]
    new_imag = keep_rate * spectral[:, 1] + mix_rate * spectral[:, 0]
    back_cos, back_sin = circle(full_z, full_z, full_z, 1.0)
    part_real, part_imag = contract("yqk,qz->yzk", new_real, new_imag, back_cos, back_sin)
    returning = jnp.stack([part_real, part_imag], 1)
    own_planes = lax.all_to_all(returning, "section", split_axis=2, concat_axis=0, tiled=True)
    grid_real = own_planes[:, 0].reshape(y_block, plane_count, blocks_x, 128)
    grid_imag = own_planes[:, 1].reshape(y_block, plane_count, blocks_x, 128)
    lane_cos, lane_sin = circle(128, 128, 128, 1.0)
    part_real, part_imag = contract("szjk,kb->szjb", grid_real, grid_imag, lane_cos, lane_sin)
    twist_cos, twist_sin = circle(full_x, blocks_x, 128, 1.0)
    part_real, part_imag = rotate(part_real, part_imag, twist_cos, twist_sin)
    first_cos, first_sin = circle(blocks_x, blocks_x, blocks_x, 1.0)
    part_real, part_imag = contract("szjb,ja->absz", part_real, part_imag, first_cos, first_sin)
    leaving = jnp.stack([part_real, part_imag], 0).reshape(2, full_x, 1, y_block * plane_count)
    rows_back = lax.all_to_all(leaving, "slab", split_axis=1, concat_axis=2, tiled=True)
    rows_back = rows_back.reshape(2, row_count, blocks_y, 128, plane_count)
    part_real, part_imag = contract("xjkz,kb->xjbz", rows_back[0], rows_back[1], lane_cos, lane_sin)
    twist_cos, twist_sin = circle(full_y, blocks_y, 128, 1.0)
    part_real, part_imag = rotate(
        part_real, part_imag, twist_cos[:, :, None], twist_sin[:, :, None]
    )
    first_cos, first_sin = circle(blocks_y, blocks_y, blocks_y, 1.0)
    new_field = real_only("xjbz,ja->zxab", part_real, part_imag, first_cos, first_sin)
    new_field = new_field.reshape(plane_count, row_count, full_y) / cell_count
    total_bulk = lax.psum(bulk_sum, ("section", "slab"))
    energy = total_bulk / cell_count
    return (new_field, energy)


lanes = 128
row_group = 32
groups = 8
kk = 8
vmem_limit = 48 * 1024 * 1024
small_limit = 8 * 1024 * 1024


def split(values):
    high = values.astype(jnp.bfloat16)
    low = (values - high.astype(jnp.float32)).astype(jnp.bfloat16)
    return high, low


def triple(left_parts, right_parts, dims):
    def product(left, right):
        return lax.dot_general(left, right, (dims, ((), ())), preferred_element_type=jnp.float32)

    left_high, left_low = left_parts
    right_high, right_low = right_parts
    return (
        product(left_high, right_high)
        + product(left_low, right_high)
        + product(left_high, right_low)
    )


def y_tables(full_y, devices, parity):
    half = full_y // 2
    per_part = half // 2 // devices
    slot = np.arange(half)
    device, inner = slot // (2 * per_part), slot % (2 * per_part)
    part, local = inner // per_part, inner % per_part
    wave = parity + 2 * (device * per_part + local)
    position = np.arange(half)
    turns = wave[:, None] * position[None, :] % full_y
    phase = turns * (2.0 * math.pi / full_y)
    coarse = phase[::row_group]
    offset = wave[:row_group] - wave[0]
    fine = (offset[:, None] * position[None, :] % full_y) * (2.0 * math.pi / full_y)
    fine = fine + part[:row_group, None] * (0.5 * math.pi)
    return [
        table.astype(np.float32)
        for table in (np.cos(coarse), np.sin(coarse), np.cos(fine), np.sin(fine))
    ]


def y_block(refs, block, parity, kk):
    coarse_cos, coarse_sin, fine_cos, fine_sin = refs
    cos_fine, sin_fine = fine_cos[...], fine_sin[...]
    pieces = []
    for inner in range(groups):
        at = pl.ds(block * groups + inner, 1)
        piece = coarse_cos[at, :] * cos_fine - coarse_sin[at, :] * sin_fine
        if parity == 0 and inner == 0:
            row = lax.broadcasted_iota(jnp.int32, piece.shape, 0)
            column = lax.broadcasted_iota(jnp.int32, piece.shape, 1)
            sign = 1.0 - 2.0 * (column % 2).astype(jnp.float32)
            wanted = jnp.where(block == 0, kk, -1)
            piece = jnp.where(row == wanted, sign, piece)
        pieces.append(piece)
    return jnp.concatenate(pieces, 0)


def times_unit(real, imag, quarter_turns):
    turns = quarter_turns % 4
    if turns == 0:
        return real, imag
    if turns == 1:
        return -imag, real
    if turns == 2:
        return -real, -imag
    return imag, -real


def unit_sum(parts, power, direction):
    total_real, total_imag = parts[0]
    for index in range(1, len(parts)):
        real, imag = times_unit(*parts[index], direction * power * index)
        total_real = total_real + real
        total_imag = total_imag + imag
    return total_real, total_imag


def flip(bit, wanted):
    return 1 - bit if wanted else bit


class Place:
    def __init__(self):
        self.section = lax.axis_index("section")
        self.slab = lax.axis_index("slab")
        self.upper = self.slab // 8
        self.bits = [self.slab % 2, self.slab // 2 % 2, self.slab // 4 % 2, self.section]
        self.member = self.index_of(self.bits)

    @staticmethod
    def index_of(bits):
        return bits[3] * 8 + bits[2] * 4 + bits[1] * 2 + bits[0]

    def peer(self, turn):
        bits = [flip(bit, turn >> at & 1) for at, bit in enumerate(self.bits)]
        slab = self.upper * 8 + bits[2] * 4 + bits[1] * 2 + bits[0]
        return self.index_of(bits), (bits[3], slab)

    def partner(self):
        return self.section, (1 - self.upper) * 8 + self.slab % 8


def remote(source, target, send, receive, device):
    return pltpu.make_async_remote_copy(
        src_ref=source,
        dst_ref=target,
        send_sem=send,
        recv_sem=receive,
        device_id=device,
        device_id_type=pl.DeviceIdType.MESH,
    )


turn_order = list(range(1, 16))


def greet(place):
    barrier = pltpu.get_barrier_semaphore()
    devices = [place.peer(turn)[1] for turn in turn_order] + [place.partner()]
    for device in devices:
        pl.semaphore_signal(
            barrier, inc=1, device_id=device, device_id_type=pl.DeviceIdType.MESH
        )
    return lambda: pl.semaphore_wait(barrier, len(devices))


def step_kernel(cells, chunks, conc_from, y_from, x_from, *refs):
    even_ref, odd_ref, energy_ref = refs[0:3]
    (
        conc_ref, y_ref, x_ref, loaded,
        high_ref, low_ref, wide_high, wide_low, spec_ref, fil_ref,
        sent_ref, arrived_ref, own_ref, other_ref, partner_ref, returned_ref,
        tile_ref, half_ref, far_ref,
        sent_out, sent_in, other_out, other_in, own_out, own_in, tile_out, tile_in,
        half_out, half_in,
    ) = refs[3:]
    loads = [
        pltpu.make_async_copy(conc_from, conc_ref, loaded.at[0]),
        pltpu.make_async_copy(y_from.at[1], y_ref.at[1], loaded.at[1]),
        pltpu.make_async_copy(x_from, x_ref, loaded.at[2]),
        pltpu.make_async_copy(y_from.at[0], y_ref.at[0], loaded.at[3]),
    ]
    for load in loads:
        load.start()
    tables = [[y_ref.at[parity, at] for at in range(4)] for parity in range(2)]
    x_rows = x_ref.shape[0]
    short = row_group // 2
    starts = [0, 8, 16, 24, 24 + short, 24 + 2 * short, 24 + 2 * short + row_group]
    ends = starts[1:] + [x_rows]
    wx_ref, tw_cos, tw_sin, ca, sa, cb, sb = [
        x_ref.at[slice(start, end)] for start, end in zip(starts, ends)
    ]
    place = Place()
    member = place.member
    planes, rows, full_y = conc_ref.shape
    half = full_y // 2
    members, inner, columns = arrived_ref.shape[1:]
    width = spec_ref.shape[4]
    sections = 2
    full_z = planes * sections
    zf_local = planes * 2
    total_zf = zf_local * sections
    slabs = members // sections
    quarter = slabs // 2
    met = greet(place)

    def prepare(parity, wants_bulk):
        total = jnp.zeros((8, lanes), jnp.float32)
        for plane in range(planes):
            first = conc_ref[plane, :, :half]
            second = conc_ref[plane, :, half:]
            first_sq, second_sq = first * first, second * second
            if wants_bulk:
                bulk = 0.25 * (first_sq * first_sq + second_sq * second_sq)
                bulk = bulk - 0.5 * (first_sq + second_sq)
                bulk = jnp.sum(bulk.reshape(rows // 8, 8, half), axis=0)
                for at in range(0, half, lanes):
                    total = total + bulk[:, at : at + lanes]
            first_g = first_sq * first - first
            second_g = second_sq * second - second
            for field, (left, right) in enumerate(((first, second), (first_g, second_g))):
                mixed = left + right if parity == 0 else left - right
                high, low = split(mixed)
                at = (plane * 2 + field) * rows
                high_ref[at : at + rows, :] = high
                low_ref[at : at + rows, :] = low
        return total

    def forward(parity, sub, at):
        table = y_block(tables[parity], sub, parity, kk)
        result = triple(split(table), (high_ref[...], low_ref[...]), ((1,), (1,)))
        sent_ref[at] = result.reshape(members, inner, columns)
        arrived_ref[at, member] = sent_ref[at, member]

    def spread(at):
        copies = []
        for turn in turn_order:
            peer, device = place.peer(turn)
            copies.append(
                remote(
                    sent_ref.at[at, peer],
                    arrived_ref.at[at, member],
                    sent_out.at[at, turn],
                    sent_in.at[at, turn],
                    device,
                )
            )
        return copies

    def spread_tile():
        copies = []
        for turn in turn_order:
            copies.append(
                remote(
                    tile_ref.at[member],
                    tile_ref.at[member],
                    tile_out.at[turn],
                    tile_in.at[turn],
                    place.peer(turn)[1],
                )
            )
        return copies

    def wide_table():
        cos_rows, sin_rows = [], []
        cos_fine, sin_fine = cb[...], sb[...]
        for group in range(row_group // 2):
            cos_base, sin_base = ca[group : group + 1, :], sa[group : group + 1, :]
            cos_rows.append(cos_base * cos_fine - sin_base * sin_fine)
            sin_rows.append(sin_base * cos_fine + cos_base * sin_fine)
        table = jnp.concatenate([jnp.concatenate(cos_rows, 0), jnp.concatenate(sin_rows, 0)], 1)
        wide_high[...], wide_low[...] = split(table)

    def middle(chunk, has_extra):
        depth = 2 * kk if has_extra else kk
        sub = lax.rem(chunk, len(chunks) // 2)
        parity = jnp.where(chunk < len(chunks) // 2, 1, 0)
        base_wave = parity + 2 * kk * (sub * members + member)
        row_iota = lax.broadcasted_iota(jnp.int32, (kk, 1), 0)
        special = None
        if has_extra:
            wanted = jnp.where(member == 0, 0, -1)
            special = jnp.where(row_iota == wanted, 1.0, 0.0)

        def gather(section, a, part, zf):
            pieces = [
                arrived_ref[
                    chunk,
                    section * slabs + a * quarter + step,
                    part * kk : (part + 1) * kk,
                    zf * lanes : (zf + 1) * lanes,
                ]
                for step in range(quarter)
            ]
            return jnp.concatenate(pieces, 1)

        def put(parts, at, row):
            for j in range(4):
                real, imag = unit_sum(parts, j, -1)
                if j:
                    cos, sin = tw_cos[j : j + 1, :], tw_sin[j : j + 1, :]
                    real, imag = real * cos + imag * sin, imag * cos - real * sin
                spec_ref[j, 0, at, row : row + kk, :] = real
                spec_ref[j, 1, at, row : row + kk, :] = imag

        for section in range(sections):
            for zf in range(zf_local):
                at = section * zf_local + zf
                parts, extra = [], []
                for a in range(2):
                    real, imag = gather(section, a, 0, zf), gather(section, a, 1, zf)
                    if has_extra:
                        extra.append((imag * special, jnp.zeros_like(imag)))
                        imag = imag * (1.0 - special)
                    parts.append((real, imag))
                put(parts, at, 0)
                if has_extra:
                    put(extra, at, kk)

        weights = (wide_high[...], wide_low[...])

        def one(pair, carry):
            source = spec_ref[pl.ds(2 * pair, 2), :, :, 0:depth, :]
            raw = triple(split(source.reshape(4 * total_zf * depth, width)), weights, ((1,), (0,)))
            raw = raw.reshape(2, 2, total_zf, depth, 2 * width)
            for inside in range(2):
                j = 2 * pair + inside
                for row in range(0, depth, kk):
                    fields = []
                    for field in range(2):
                        per_z = []
                        for z in range(full_z):
                            re_part = raw[inside, 0, z * 2 + field, row : row + kk]
                            im_part = raw[inside, 1, z * 2 + field, row : row + kk]
                            per_z.append(
                                (
                                    re_part[:, :width] + im_part[:, width:],
                                    im_part[:, :width] - re_part[:, width:],
                                )
                            )
                        fields.append(per_z)
                    wave = base_wave + 2 * row_iota
                    if row:
                        wave = jnp.full_like(wave, half)
                    first = (wave == 0) | (wave == half)
                    weight = jnp.where(first, 1.0 / cells, 2.0 / cells)
                    angle = wave.astype(jnp.float32) * (2.0 * math.pi / full_y)
                    plane_sq = angle * angle + wx_ref[pl.ds(j, 1), :]
                    updated = []
                    for q in range(full_z):
                        c_real, c_imag = unit_sum(fields[0], q, -1)
                        g_real, g_imag = unit_sum(fields[1], q, -1)
                        signed = q - full_z if 2 * q >= full_z else q
                        wave_sq = plane_sq + (2.0 * math.pi * signed / full_z) ** 2
                        numerator = 1.0 + time_step * stabilizer * wave_sq
                        denominator = numerator + time_step * kappa_grad * wave_sq * wave_sq
                        inverse = weight / denominator
                        keep = numerator * inverse
                        mix = time_step * wave_sq * inverse
                        updated.append(
                            (keep * c_real - mix * g_real, keep * c_imag - mix * g_imag)
                        )
                    for z in range(full_z):
                        real, imag = unit_sum(updated, z, 1)
                        fil_ref[j, 0, z, row : row + kk, :] = real
                        fil_ref[j, 1, z, row : row + kk, :] = imag
            return carry

        lax.fori_loop(0, 2, one, 0)
        source = fil_ref[:, :, :, 0:depth, :].reshape(8 * full_z * depth, width)
        raw = triple(split(source), weights, ((1,), (0,))).reshape(4, 2, full_z, depth, 2 * width)

        def back(z, row):
            parts = []
            for j in range(4):
                re_part = raw[j, 0, z, row : row + kk]
                im_part = raw[j, 1, z, row : row + kk]
                real = re_part[:, :width] - im_part[:, width:]
                imag = re_part[:, width:] + im_part[:, :width]
                if j:
                    cos, sin = tw_cos[j : j + 1, :], tw_sin[j : j + 1, :]
                    real, imag = real * cos - imag * sin, imag * cos + real * sin
                parts.append((real, imag))
            return parts

        for z in range(full_z):
            section, plane = z // planes, z % planes
            parts = back(z, 0)
            extra = back(z, kk) if has_extra else None
            for a in range(4):
                real, imag = unit_sum(parts, a, 1)
                if has_extra:
                    extra_real, _ = unit_sum(extra, a, 1)
                    imag = imag * (1.0 - special) + extra_real * special
                target_ref = own_ref if a < 2 else other_ref
                for step in range(quarter):
                    target = section * slabs + a % 2 * quarter + step
                    piece = slice(step * lanes, (step + 1) * lanes)
                    at = plane * inner
                    target_ref[chunk, target, at : at + kk, :] = real[:, piece]
                    target_ref[chunk, target, at + kk : at + 2 * kk, :] = imag[:, piece]

    def cross(chunk):
        return remote(
            other_ref.at[chunk],
            partner_ref.at[chunk],
            other_out.at[chunk],
            other_in.at[chunk],
            place.partner(),
        )

    def far():
        return remote(half_ref, far_ref, half_out, half_in, place.partner())

    def join(chunk):
        wait_in([cross(chunk)])
        own_ref[chunk] = own_ref[chunk] + partner_ref[chunk]
        returned_ref[chunk, member] = own_ref[chunk, member]
        start(give_back(chunk))

    def give_back(chunk):
        copies = []
        for turn in turn_order:
            peer, device = place.peer(turn)
            copies.append(
                remote(
                    own_ref.at[chunk, peer],
                    returned_ref.at[chunk, member],
                    own_out.at[chunk, turn],
                    own_in.at[chunk, turn],
                    device,
                )
            )
        return copies

    def backward(parity, sub, chunk):
        turned = [
            returned_ref[chunk, :, plane * inner : (plane + 1) * inner, :]
            .reshape(members * inner, rows)
            .T
            for plane in range(planes)
        ]
        table = y_block(tables[parity], sub, parity, kk)
        term = triple(split(jnp.concatenate(turned, 0)), split(table), ((1,), (0,)))
        target = (even_ref, odd_ref)[parity]
        target[...] = target[...] + term

    def start(copies):
        for copy in copies:
            copy.start()

    def wait_in(copies):
        for copy in copies:
            copy.wait_recv()

    total = len(chunks)
    special_at = chunks.index((0, 0))
    subs = total // 2
    lead = 2
    even_ref[...] = jnp.zeros_like(even_ref)
    odd_ref[...] = jnp.zeros_like(odd_ref)
    loads[0].wait()
    tile_ref[member] = prepare(1, True)
    loads[1].wait()
    forward(1, 0, 0)
    met()
    start(spread(0))
    start(spread_tile())
    forward(1, 1, 1)
    start(spread(1))
    loads[2].wait()
    wide_table()
    lax.fori_loop(2, subs, lambda at, carry: forward(1, at, at), None)
    prepare(0, False)
    loads[3].wait()
    lax.fori_loop(0, subs, lambda at, carry: forward(0, at, subs + at), None)

    def one(at, carry):
        wait_in(spread(at))

        @pl.when(at != special_at)
        def _():
            middle(at, False)

        @pl.when(at == special_at)
        def _():
            middle(at, True)

        start([cross(at)])

        @pl.when(at + lead < total)
        def _():
            start(spread(at + lead))

        @pl.when(at == 0)
        def _():
            wait_in(spread_tile())
            half_ref[...] = jnp.sum(tile_ref[...], axis=0)
            start([far()])

        @pl.when(at >= 2)
        def _():
            join(at - 2)

        @pl.when(at >= subs)
        def _():
            wait_in(give_back(at - subs))
            backward(1, at - subs, at - subs)

        return carry

    lax.fori_loop(0, total, one, 0)
    wait_in([far()])
    energy_ref[0, 0] = jnp.sum(half_ref[...] + far_ref[...]) / cells

    def last(at, carry):
        @pl.when(at < 2)
        def _():
            join(at + total - 2)

        wait_in(give_back(at + subs))
        backward(0, at, at + subs)
        return carry

    lax.fori_loop(0, subs, last, 0)

    def sent(at, carry):
        for copy in spread(at) + give_back(at) + [cross(at)]:
            copy.wait_send()
        return carry

    lax.fori_loop(0, total, sent, 0)
    for copy in spread_tile() + [far()]:
        copy.wait_send()


def combine_kernel(even_ref, odd_ref, out_ref):
    planes, rows, full_y = out_ref.shape
    half = full_y // 2
    for plane in range(planes):
        even_rows = even_ref[plane * rows : (plane + 1) * rows, :]
        odd_rows = odd_ref[plane * rows : (plane + 1) * rows, :]
        out_ref[plane, :, :half] = even_rows + odd_rows
        out_ref[plane, :, half:] = even_rows - odd_rows


def kernel_step(concentration):
    planes, rows, full_y = concentration.shape
    slabs = lax.axis_size("slab")
    sections = lax.axis_size("section")
    members = slabs * sections // 2
    full_x = rows * slabs
    full_z = planes * sections
    cells = full_x * full_y * full_z
    half = full_y // 2
    subs = half // 2 // members // kk
    width = full_x // 4
    base = np.arange(width)
    step = 2.0 * math.pi / width
    coarse = base[::row_group, None] * base[None, :] % width * step
    fine = base[:row_group, None] * base[None, :] % width * step
    dft = [f(t).astype(np.float32) for t in (coarse, fine) for f in (np.cos, np.sin)]
    twist = np.arange(4)[:, None] * base[None, :] * (2.0 * math.pi / full_x)
    twist_cos, twist_sin = np.cos(twist).astype(np.float32), np.sin(twist).astype(np.float32)
    kx = np.arange(4)[:, None] + 4 * base[None, :]
    kx = np.where(2 * kx >= full_x, kx - full_x, kx) * (2.0 * math.pi / full_x)
    wave_x = (kx * kx).astype(np.float32)
    tables = [y_tables(full_y, members * subs, parity) for parity in range(2)]
    chunks = [(1, sub) for sub in range(subs)] + [(0, sub) for sub in range(subs)]
    count = len(chunks)
    columns = planes * 2 * rows
    y_rows = np.stack([np.stack(parts) for parts in tables])
    small = [np.concatenate([rows, rows]) for rows in (wave_x, twist_cos, twist_sin)]
    coarse_cos, coarse_sin, fine_cos, fine_sin = dft
    x_rows = np.concatenate([*small, coarse_cos, coarse_sin, fine_cos, fine_sin])
    operands = [concentration, y_rows, x_rows]
    f32, bf16 = jnp.float32, jnp.bfloat16
    vmem, dma = pltpu.VMEM, pltpu.SemaphoreType.DMA
    in_vmem = pl.BlockSpec(memory_space=pltpu.VMEM)
    forth = vmem((count, members, 2 * kk, columns), f32)
    half_back = vmem((count, members, 2 * kk * planes, rows), f32)
    even, odd, energy = pl.pallas_call(
        functools.partial(step_kernel, cells, chunks),
        out_shape=(
            jax.ShapeDtypeStruct((planes * rows, half), f32),
            jax.ShapeDtypeStruct((planes * rows, half), f32),
            jax.ShapeDtypeStruct((1, 1), f32),
        ),
        in_specs=[pl.BlockSpec(memory_space=pltpu.HBM)] * len(operands),
        out_specs=(in_vmem, in_vmem, pl.BlockSpec(memory_space=pltpu.SMEM)),
        scratch_shapes=[
            vmem(concentration.shape, f32),
            vmem(y_rows.shape, f32),
            vmem(x_rows.shape, f32),
            dma((4,)),
            vmem((columns, half), bf16),
            vmem((columns, half), bf16),
            vmem((width, 2 * width), bf16),
            vmem((width, 2 * width), bf16),
            vmem((4, 2, 2 * full_z, 2 * kk, width), f32),
            vmem((4, 2, full_z, 2 * kk, width), f32),
            forth,
            forth,
            half_back,
            half_back,
            half_back,
            half_back,
            vmem((members, 8, lanes), f32),
            vmem((8, lanes), f32),
            vmem((8, lanes), f32),
            dma((count, members)),
            dma((count, members)),
            dma((count,)),
            dma((count,)),
            dma((count, members)),
            dma((count, members)),
            dma((members,)),
            dma((members,)),
            dma,
            dma,
        ],
        compiler_params=pltpu.CompilerParams(
            vmem_limit_bytes=vmem_limit, collective_id=0, has_side_effects=True
        ),
    )(*[pltpu.with_memory_space_constraint(jnp.asarray(x), pltpu.HBM) for x in operands])
    new_field = pl.pallas_call(
        combine_kernel,
        out_shape=jax.ShapeDtypeStruct(concentration.shape, f32),
        in_specs=[in_vmem] * 2,
        out_specs=in_vmem,
        compiler_params=pltpu.CompilerParams(vmem_limit_bytes=small_limit),
    )(even, odd)
    return (new_field, energy.reshape(()))


def per_device(concentration):
    planes, rows, full_y = concentration.shape
    devices = lax.axis_size("slab") * lax.axis_size("section")
    share = full_y // 4 // devices
    fits = (
        rows == lanes
        and planes * lax.axis_size("section") == 4
        and share == 2 * kk
        and devices == 32
        and lax.axis_size("section") == 2
    )
    return kernel_step(concentration) if fits else plain_step(concentration)


def solution(mesh):
    return jax.shard_map(
        per_device,
        mesh=mesh,
        in_specs=(P("section", "slab", None),),
        out_specs=(P("section", "slab", None), P()),
        check_vma=False,
    )
```

time: 147 us -> 134 us (0.912)
  Pallas kernels: 142 us -> 132 us
  local copies, waits for them, and re-layouts: 3.14 us -> 0 us
    pallas_call x1 -> x2, Pallas kernels: 142 us -> 132 us  [the longest x1 130 us: kernel_step(): pl.pallas_call(functools.partial(step_kernel, cells, chunks), out_shape=(...]
    unnamed x1 -> x0, local copies, waits for them, and re-layouts: 3.14 us -> none
where the time goes in v2:
time: 134 us
  Pallas kernels  132 us (99%)
  between operations  2.33 us (2%)
    pallas_call x1, Pallas kernels, kernel_step(): pl.pallas_call(functools.partial(step_kernel, cells, chunks), out_shape=(...  130 us

profile of v2, /device:TPU:0, one launch (start us, length us, event | category | flops | bytes accessed | tf_op | source)
XLA Modules:
  0.0 134.1 jit_solution(17577017374772440020)
XLA Ops:
  0.6 130.3 %shard_map.50 = (f32[256,1024]{1,0:T(8,128)S(1)}, f32[256,1024]{1,0:T(8,128)S(1)}, f32[1,1]{1,0:T(1,128)}) custom-call(f32[2,128,2048]{2,1,0:T(8,128)} %conc_from.1, f32[2,4,32,1024]{3,2,1,0:T(8,128)} %constant.4.clone.y_from, f32[120,512]{1,0:T(8,128)} %constant.5.clone.x_from), custom_call_target="tpu_custom_call" | custom-call | tf_op jit(solution)/shard_map/pallas_call | solution.py:698
  130.9 1.5 %shard_map.51 = f32[2,128,2048]{2,1,0:T(8,128)} custom-call(f32[256,1024]{1,0:T(8,128)S(1)} %get-tuple-element.5.even_ref, f32[256,1024]{1,0:T(8,128)S(1)} %get-tuple-element.6.odd_ref), custom_call_target="tpu_custom_call" | custom-call | tf_op jit(solution)/shard_map/pallas_call | solution.py:742

commit v3 on v2

--- a/solution.py
+++ b/solution.py
@@ -356,8 +356,8 @@
                 remote(
                     sent_ref.at[at, peer],
                     arrived_ref.at[at, member],
-                    sent_out.at[at, turn],
-                    sent_in.at[at, turn],
+                    sent_out.at[at],
+                    sent_in.at[at],
                     device,
                 )
             )
@@ -370,8 +370,8 @@
                 remote(
                     tile_ref.at[member],
                     tile_ref.at[member],
-                    tile_out.at[turn],
-                    tile_in.at[turn],
+                    tile_out,
+                    tile_in,
                     place.peer(turn)[1],
                 )
             )
@@ -529,7 +529,7 @@
         return remote(half_ref, far_ref, half_out, half_in, place.partner())
 
     def join(chunk):
-        wait_in([cross(chunk)])
+        cross(chunk).wait_recv()
         own_ref[chunk] = own_ref[chunk] + partner_ref[chunk]
         returned_ref[chunk, member] = own_ref[chunk, member]
         start(give_back(chunk))
@@ -542,8 +542,8 @@
                 remote(
                     own_ref.at[chunk, peer],
                     returned_ref.at[chunk, member],
-                    own_out.at[chunk, turn],
-                    own_in.at[chunk, turn],
+                    own_out.at[chunk],
+                    own_in.at[chunk],
                     device,
                 )
             )
@@ -561,13 +561,31 @@
         target = (even_ref, odd_ref)[parity]
         target[...] = target[...] + term
 
+    def spread_all(at):
+        return remote(
+            sent_ref.at[at, 0 : members - 1],
+            arrived_ref.at[at, 0 : members - 1],
+            sent_out.at[at],
+            sent_in.at[at],
+            place.partner(),
+        )
+
+    def tile_all():
+        part = tile_ref.at[0 : members - 1]
+        return remote(part, part, tile_out, tile_in, place.partner())
+
+    def back_all(at):
+        return remote(
+            own_ref.at[at, 0 : members - 1],
+            returned_ref.at[at, 0 : members - 1],
+            own_out.at[at],
+            own_in.at[at],
+            place.partner(),
+        )
+
     def start(copies):
         for copy in copies:
             copy.start()
-
-    def wait_in(copies):
-        for copy in copies:
-            copy.wait_recv()
 
     total = len(chunks)
     special_at = chunks.index((0, 0))
@@ -583,16 +601,16 @@
     start(spread(0))
     start(spread_tile())
     forward(1, 1, 1)
-    start(spread(1))
     loads[2].wait()
     wide_table()
     lax.fori_loop(2, subs, lambda at, carry: forward(1, at, at), None)
+    start(spread(1))
     prepare(0, False)
     loads[3].wait()
     lax.fori_loop(0, subs, lambda at, carry: forward(0, at, subs + at), None)
 
     def one(at, carry):
-        wait_in(spread(at))
+        spread_all(at).wait_recv()
 
         @pl.when(at != special_at)
         def _():
@@ -610,7 +628,7 @@
 
         @pl.when(at == 0)
         def _():
-            wait_in(spread_tile())
+            tile_all().wait_recv()
             half_ref[...] = jnp.sum(tile_ref[...], axis=0)
             start([far()])
 
@@ -620,13 +638,13 @@
 
         @pl.when(at >= subs)
         def _():
-            wait_in(give_back(at - subs))
+            back_all(at - subs).wait_recv()
             backward(1, at - subs, at - subs)
 
         return carry
 
     lax.fori_loop(0, total, one, 0)
-    wait_in([far()])
+    far().wait_recv()
     energy_ref[0, 0] = jnp.sum(half_ref[...] + far_ref[...]) / cells
 
     def last(at, carry):
@@ -634,19 +652,19 @@
         def _():
             join(at + total - 2)
 
-        wait_in(give_back(at + subs))
+        back_all(at + subs).wait_recv()
         backward(0, at, at + subs)
         return carry
 
     lax.fori_loop(0, subs, last, 0)
 
     def sent(at, carry):
-        for copy in spread(at) + give_back(at) + [cross(at)]:
+        for copy in (spread_all(at), back_all(at), cross(at)):
             copy.wait_send()
         return carry
 
     lax.fori_loop(0, total, sent, 0)
-    for copy in spread_tile() + [far()]:
+    for copy in (tile_all(), far()):
         copy.wait_send()
 
 
@@ -724,14 +742,9 @@
             vmem((members, 8, lanes), f32),
             vmem((8, lanes), f32),
             vmem((8, lanes), f32),
-            dma((count, members)),
-            dma((count, members)),
-            dma((count,)),
-            dma((count,)),
-            dma((count, members)),
-            dma((count, members)),
-            dma((members,)),
-            dma((members,)),
+            *[dma((count,))] * 6,
+            dma,
+            dma,
             dma,
             dma,
         ],

time: 134 us -> 129 us (0.963)
  Pallas kernels: 132 us -> 127 us
    pallas_call x1, Pallas kernels: 130 us -> 125 us  [kernel_step(): pl.pallas_call(functools.partial(step_kernel, cells, chunks), out_shape=(...]
where the time goes in v3:
time: 129 us
  Pallas kernels  127 us (98%)
  between operations  2.33 us (2%)
    pallas_call x1, Pallas kernels, kernel_step(): pl.pallas_call(functools.partial(step_kernel, cells, chunks), out_shape=(...  125 us

profile of v3, /device:TPU:0, one launch (start us, length us, event | category | flops | bytes accessed | tf_op | source)
XLA Modules:
  0.0 129.1 jit_solution(17298569801517345477)
XLA Ops:
  0.6 125.4 %shard_map.50 = (f32[256,1024]{1,0:T(8,128)S(1)}, f32[256,1024]{1,0:T(8,128)S(1)}, f32[1,1]{1,0:T(1,128)}) custom-call(f32[2,128,2048]{2,1,0:T(8,128)} %conc_from.1, f32[2,4,32,1024]{3,2,1,0:T(8,128)} %constant.4.clone.y_from, f32[120,512]{1,0:T(8,128)} %constant.5.clone.x_from), custom_call_target="tpu_custom_call" | custom-call | tf_op jit(solution)/shard_map/pallas_call | solution.py:716
  126.0 1.5 %shard_map.51 = f32[2,128,2048]{2,1,0:T(8,128)} custom-call(f32[256,1024]{1,0:T(8,128)S(1)} %get-tuple-element.5.even_ref, f32[256,1024]{1,0:T(8,128)S(1)} %get-tuple-element.6.odd_ref), custom_call_target="tpu_custom_call" | custom-call | tf_op jit(solution)/shard_map/pallas_call | solution.py:755

commit v4 on v3

--- a/solution.py
+++ b/solution.py
@@ -240,20 +240,25 @@
         self.section = lax.axis_index("section")
         self.slab = lax.axis_index("slab")
         self.upper = self.slab // 8
-        self.bits = [self.slab % 2, self.slab // 2 % 2, self.slab // 4 % 2, self.section]
-        self.member = self.index_of(self.bits)
-
-    @staticmethod
-    def index_of(bits):
-        return bits[3] * 8 + bits[2] * 4 + bits[1] * 2 + bits[0]
+        depth = self.slab // 4 % 2
+        self.inner = depth + self.upper - 2 * depth * self.upper
+        self.bits = [self.slab % 2, self.slab // 2 % 2, 1 - self.inner, self.section]
+        self.here = self.indices(self.bits)
+
+    def indices(self, bits):
+        inner = 1 - bits[2]
+        depth = inner + self.upper - 2 * inner * self.upper
+        low = bits[1] * 2 + bits[0]
+        by_rows = bits[3] * 8 + depth * 4 + low
+        by_waves = bits[3] * 8 + inner * 4 + low
+        among_inner = bits[3] * 4 + low
+        return by_rows, by_waves, among_inner, (bits[3], self.upper * 8 + depth * 4 + low)
 
     def peer(self, turn):
-        bits = [flip(bit, turn >> at & 1) for at, bit in enumerate(self.bits)]
-        slab = self.upper * 8 + bits[2] * 4 + bits[1] * 2 + bits[0]
-        return self.index_of(bits), (bits[3], slab)
+        return self.indices([flip(bit, turn >> at & 1) for at, bit in enumerate(self.bits)])
 
     def partner(self):
-        return self.section, (1 - self.upper) * 8 + self.slab % 8
+        return self.section, 12 - self.slab // 4 * 4 + self.slab % 4
 
 
 def remote(source, target, send, receive, device):
@@ -267,12 +272,15 @@
     )
 
 
+same_side = [turn for turn in range(1, 16) if not turn & 4]
+other_side = [turn for turn in range(1, 16) if turn & 4]
 turn_order = list(range(1, 16))
+lead, lag, wait_lag = 5, 2, 6
 
 
 def greet(place):
     barrier = pltpu.get_barrier_semaphore()
-    devices = [place.peer(turn)[1] for turn in turn_order] + [place.partner()]
+    devices = [place.peer(turn)[3] for turn in turn_order] + [place.partner()]
     for device in devices:
         pl.semaphore_signal(
             barrier, inc=1, device_id=device, device_id_type=pl.DeviceIdType.MESH
@@ -307,10 +315,12 @@
         x_ref.at[slice(start, end)] for start, end in zip(starts, ends)
     ]
     place = Place()
-    member = place.member
+    by_rows, by_waves, among_inner, _ = place.here
+    is_inner = place.inner == 1
     planes, rows, full_y = conc_ref.shape
     half = full_y // 2
     members, inner, columns = arrived_ref.shape[1:]
+    items = arrived_ref.shape[0]
     width = spec_ref.shape[4]
     sections = 2
     full_z = planes * sections
@@ -346,33 +356,58 @@
         table = y_block(tables[parity], sub, parity, kk)
         result = triple(split(table), (high_ref[...], low_ref[...]), ((1,), (1,)))
         sent_ref[at] = result.reshape(members, inner, columns)
-        arrived_ref[at, member] = sent_ref[at, member]
-
-    def spread(at):
+
+    def shared(item):
+        return lax.rem(item, 3) == 0
+
+    def takes(item):
+        return shared(item) | is_inner
+
+    def chunk_of(item):
+        return item // 3 * 2 + jnp.where(shared(item), 0, 1)
+
+    def slot_of(item, waves, order):
+        return jnp.where(shared(item), waves, 2 * order + lax.rem(item, 3) - 1)
+
+    def copies_out(item, turns):
         copies = []
-        for turn in turn_order:
-            peer, device = place.peer(turn)
+        for turn in turns:
+            _, waves, order, device = place.peer(turn)
             copies.append(
                 remote(
-                    sent_ref.at[at, peer],
-                    arrived_ref.at[at, member],
-                    sent_out.at[at],
-                    sent_in.at[at],
+                    sent_ref.at[chunk_of(item), slot_of(item, waves, order)],
+                    arrived_ref.at[item, by_rows],
+                    sent_out.at[item],
+                    sent_in.at[item],
                     device,
                 )
             )
         return copies
+
+    def spread(item):
+        @pl.when(shared(item) | is_inner)
+        def _():
+            start(copies_out(item, same_side))
+
+        @pl.when(shared(item) | ~is_inner)
+        def _():
+            start(copies_out(item, other_side))
+
+        @pl.when(takes(item))
+        def _():
+            slot = slot_of(item, by_waves, among_inner)
+            arrived_ref[item, by_rows] = sent_ref[chunk_of(item), slot]
 
     def spread_tile():
         copies = []
         for turn in turn_order:
             copies.append(
                 remote(
-                    tile_ref.at[member],
-                    tile_ref.at[member],
+                    tile_ref.at[by_rows],
+                    tile_ref.at[by_rows],
                     tile_out,
                     tile_in,
-                    place.peer(turn)[1],
+                    place.peer(turn)[3],
                 )
             )
         return copies
@@ -387,21 +422,23 @@
         table = jnp.concatenate([jnp.concatenate(cos_rows, 0), jnp.concatenate(sin_rows, 0)], 1)
         wide_high[...], wide_low[...] = split(table)
 
-    def middle(chunk, has_extra):
+    def middle(item, has_extra):
         depth = 2 * kk if has_extra else kk
+        chunk = chunk_of(item)
         sub = lax.rem(chunk, len(chunks) // 2)
         parity = jnp.where(chunk < len(chunks) // 2, 1, 0)
-        base_wave = parity + 2 * kk * (sub * members + member)
+        slot = slot_of(item, by_waves, among_inner)
+        base_wave = parity + 2 * kk * (sub * members + slot)
         row_iota = lax.broadcasted_iota(jnp.int32, (kk, 1), 0)
         special = None
         if has_extra:
-            wanted = jnp.where(member == 0, 0, -1)
+            wanted = jnp.where(slot == 0, 0, -1)
             special = jnp.where(row_iota == wanted, 1.0, 0.0)
 
         def gather(section, a, part, zf):
             pieces = [
                 arrived_ref[
-                    chunk,
+                    item,
                     section * slabs + a * quarter + step,
                     part * kk : (part + 1) * kk,
                     zf * lanes : (zf + 1) * lanes,
@@ -513,41 +550,37 @@
                     target = section * slabs + a % 2 * quarter + step
                     piece = slice(step * lanes, (step + 1) * lanes)
                     at = plane * inner
-                    target_ref[chunk, target, at : at + kk, :] = real[:, piece]
-                    target_ref[chunk, target, at + kk : at + 2 * kk, :] = imag[:, piece]
-
-    def cross(chunk):
+                    target_ref[item, target, at : at + kk, :] = real[:, piece]
+                    target_ref[item, target, at + kk : at + 2 * kk, :] = imag[:, piece]
+
+    def cross(item):
         return remote(
-            other_ref.at[chunk],
-            partner_ref.at[chunk],
-            other_out.at[chunk],
-            other_in.at[chunk],
+            other_ref.at[item],
+            partner_ref.at[item],
+            other_out.at[item],
+            other_in.at[item],
             place.partner(),
         )
 
     def far():
         return remote(half_ref, far_ref, half_out, half_in, place.partner())
 
-    def join(chunk):
-        cross(chunk).wait_recv()
-        own_ref[chunk] = own_ref[chunk] + partner_ref[chunk]
-        returned_ref[chunk, member] = own_ref[chunk, member]
-        start(give_back(chunk))
-
-    def give_back(chunk):
-        copies = []
-        for turn in turn_order:
-            peer, device = place.peer(turn)
-            copies.append(
+    def join(item):
+        @pl.when(takes(item))
+        def _():
+            cross(item).wait_recv()
+            chunk, slot = chunk_of(item), slot_of(item, by_waves, among_inner)
+            own_ref[item] = own_ref[item] + partner_ref[item]
+            returned_ref[chunk, slot] = own_ref[item, by_rows]
+            for turn in turn_order:
+                rows_at, _, _, device = place.peer(turn)
                 remote(
-                    own_ref.at[chunk, peer],
-                    returned_ref.at[chunk, member],
-                    own_out.at[chunk],
-                    own_in.at[chunk],
+                    own_ref.at[item, rows_at],
+                    returned_ref.at[chunk, slot],
+                    own_out.at[item],
+                    own_in.at[item],
                     device,
-                )
-            )
-        return copies
+                ).start()
 
     def backward(parity, sub, chunk):
         turned = [
@@ -561,12 +594,12 @@
         target = (even_ref, odd_ref)[parity]
         target[...] = target[...] + term
 
-    def spread_all(at):
+    def forth(item, count):
         return remote(
-            sent_ref.at[at, 0 : members - 1],
-            arrived_ref.at[at, 0 : members - 1],
-            sent_out.at[at],
-            sent_in.at[at],
+            sent_ref.at[0, 0:count],
+            arrived_ref.at[item, 0:count],
+            sent_out.at[item],
+            sent_in.at[item],
             place.partner(),
         )
 
@@ -574,98 +607,125 @@
         part = tile_ref.at[0 : members - 1]
         return remote(part, part, tile_out, tile_in, place.partner())
 
-    def back_all(at):
+    def home(item, count):
         return remote(
-            own_ref.at[at, 0 : members - 1],
-            returned_ref.at[at, 0 : members - 1],
-            own_out.at[at],
-            own_in.at[at],
+            own_ref.at[item, 0:count],
+            returned_ref.at[chunk_of(item), 0:count],
+            own_out.at[item],
+            own_in.at[item],
             place.partner(),
         )
+
+    def by_kind(item, act):
+        for count, kind in (
+            (members - 1, shared(item)),
+            (len(same_side), ~shared(item) & is_inner),
+            (len(other_side), ~shared(item) & ~is_inner),
+        ):
+
+            @pl.when(kind)
+            def _():
+                act(count)
+
+    def wait_home(chunk):
+        first = chunk // 2 * 3 + lax.rem(chunk, 2)
+        by_kind(first, lambda count: home(first, count).wait_recv())
+
+        @pl.when(lax.rem(chunk, 2) == 1)
+        def _():
+            by_kind(first + 1, lambda count: home(first + 1, count).wait_recv())
 
     def start(copies):
         for copy in copies:
             copy.start()
 
     total = len(chunks)
-    special_at = chunks.index((0, 0))
     subs = total // 2
-    lead = 2
+    special_at = chunks.index((0, 0)) // 2 * 3
     even_ref[...] = jnp.zeros_like(even_ref)
     odd_ref[...] = jnp.zeros_like(odd_ref)
     loads[0].wait()
-    tile_ref[member] = prepare(1, True)
+    tile_ref[by_rows] = prepare(1, True)
     loads[1].wait()
     forward(1, 0, 0)
     met()
-    start(spread(0))
+    spread(0)
     start(spread_tile())
     forward(1, 1, 1)
     loads[2].wait()
     wide_table()
     lax.fori_loop(2, subs, lambda at, carry: forward(1, at, at), None)
-    start(spread(1))
+    for item in range(1, lead):
+        spread(item)
     prepare(0, False)
     loads[3].wait()
     lax.fori_loop(0, subs, lambda at, carry: forward(0, at, subs + at), None)
 
-    def one(at, carry):
-        spread_all(at).wait_recv()
-
-        @pl.when(at != special_at)
-        def _():
-            middle(at, False)
-
-        @pl.when(at == special_at)
-        def _():
-            middle(at, True)
-
-        start([cross(at)])
-
-        @pl.when(at + lead < total)
-        def _():
-            start(spread(at + lead))
-
-        @pl.when(at == 0)
+    def one(item, carry):
+        @pl.when(takes(item))
+        def _():
+            forth(item, members - 1).wait_recv()
+
+            @pl.when(item != special_at)
+            def _():
+                middle(item, False)
+
+            @pl.when(item == special_at)
+            def _():
+                middle(item, True)
+
+            cross(item).start()
+
+        @pl.when(item + lead < items)
+        def _():
+            spread(item + lead)
+
+        @pl.when(item == 0)
         def _():
             tile_all().wait_recv()
             half_ref[...] = jnp.sum(tile_ref[...], axis=0)
-            start([far()])
-
-        @pl.when(at >= 2)
-        def _():
-            join(at - 2)
-
-        @pl.when(at >= subs)
-        def _():
-            back_all(at - subs).wait_recv()
-            backward(1, at - subs, at - subs)
+            far().start()
+
+        @pl.when(item >= lag)
+        def _():
+            join(item - lag)
+
+        @pl.when((item >= wait_lag) & (lax.rem(item, 3) != 1))
+        def _():
+            chunk = chunk_of(item - wait_lag)
+            wait_home(chunk)
+            backward(1, chunk, chunk)
 
         return carry
 
-    lax.fori_loop(0, total, one, 0)
+    lax.fori_loop(0, items, one, 0)
     far().wait_recv()
     energy_ref[0, 0] = jnp.sum(half_ref[...] + far_ref[...]) / cells
 
     def last(at, carry):
-        @pl.when(at < 2)
-        def _():
-            join(at + total - 2)
-
-        back_all(at + subs).wait_recv()
+        @pl.when(at < lag)
+        def _():
+            join(at + items - lag)
+
+        wait_home(at + subs)
         backward(0, at, at + subs)
         return carry
 
     lax.fori_loop(0, subs, last, 0)
 
-    def sent(at, carry):
-        for copy in (spread_all(at), back_all(at), cross(at)):
-            copy.wait_send()
+    def sent(item, carry):
+        by_kind(item, lambda count: forth(item, count).wait_send())
+
+        @pl.when(takes(item))
+        def _():
+            home(item, members - 1).wait_send()
+            cross(item).wait_send()
+
         return carry
 
-    lax.fori_loop(0, total, sent, 0)
-    for copy in (tile_all(), far()):
-        copy.wait_send()
+    lax.fori_loop(0, items, sent, 0)
+    tile_all().wait_send()
+    far().wait_send()
 
 
 def combine_kernel(even_ref, odd_ref, out_ref):
@@ -702,6 +762,7 @@
     tables = [y_tables(full_y, members * subs, parity) for parity in range(2)]
     chunks = [(1, sub) for sub in range(subs)] + [(0, sub) for sub in range(subs)]
     count = len(chunks)
+    items = count // 2 * 3
     columns = planes * 2 * rows
     y_rows = np.stack([np.stack(parts) for parts in tables])
     small = [np.concatenate([rows, rows]) for rows in (wave_x, twist_cos, twist_sin)]
@@ -711,8 +772,7 @@
     f32, bf16 = jnp.float32, jnp.bfloat16
     vmem, dma = pltpu.VMEM, pltpu.SemaphoreType.DMA
     in_vmem = pl.BlockSpec(memory_space=pltpu.VMEM)
-    forth = vmem((count, members, 2 * kk, columns), f32)
-    half_back = vmem((count, members, 2 * kk * planes, rows), f32)
+    half_back = vmem((items, members, 2 * kk * planes, rows), f32)
     even, odd, energy = pl.pallas_call(
         functools.partial(step_kernel, cells, chunks),
         out_shape=(
@@ -733,16 +793,16 @@
             vmem((width, 2 * width), bf16),
             vmem((4, 2, 2 * full_z, 2 * kk, width), f32),
             vmem((4, 2, full_z, 2 * kk, width), f32),
-            forth,
-            forth,
+            vmem((count, members, 2 * kk, columns), f32),
+            vmem((items, members, 2 * kk, columns), f32),
             half_back,
             half_back,
             half_back,
-            half_back,
+            vmem((count, members, 2 * kk * planes, rows), f32),
             vmem((members, 8, lanes), f32),
             vmem((8, lanes), f32),
             vmem((8, lanes), f32),
-            *[dma((count,))] * 6,
+            *[dma((items,))] * 6,
             dma,
             dma,
             dma,

time: 129 us -> 127 us (0.984)
  Pallas kernels: 127 us -> 124 us
    pallas_call x1, Pallas kernels: 125 us -> 123 us  [kernel_step(): pl.pallas_call(functools.partial(step_kernel, cells, chunks), out_shape=(...]
where the time goes in v4:
time: 127 us
  Pallas kernels  124 us (98%)
  between operations  2.33 us (2%)
    pallas_call x1, Pallas kernels, kernel_step(): pl.pallas_call(functools.partial(step_kernel, cells, chunks), out_shape=(...  123 us

profile of v4, /device:TPU:0, one launch (start us, length us, event | category | flops | bytes accessed | tf_op | source)
XLA Modules:
  0.0 126.6 jit_solution(3199590605492692512)
XLA Ops:
  0.6 122.8 %shard_map.50 = (f32[256,1024]{1,0:T(8,128)S(1)}, f32[256,1024]{1,0:T(8,128)S(1)}, f32[1,1]{1,0:T(1,128)}) custom-call(f32[2,128,2048]{2,1,0:T(8,128)} %conc_from.1, f32[2,4,32,1024]{3,2,1,0:T(8,128)} %constant.4.clone.y_from, f32[120,512]{1,0:T(8,128)} %constant.5.clone.x_from), custom_call_target="tpu_custom_call" | custom-call | tf_op jit(solution)/shard_map/pallas_call | solution.py:776
  123.4 1.5 %shard_map.51 = f32[2,128,2048]{2,1,0:T(8,128)} custom-call(f32[256,1024]{1,0:T(8,128)S(1)} %get-tuple-element.5.even_ref, f32[256,1024]{1,0:T(8,128)S(1)} %get-tuple-element.6.odd_ref), custom_call_target="tpu_custom_call" | custom-call | tf_op jit(solution)/shard_map/pallas_call | solution.py:815

commit v5 on v4

--- a/solution.py
+++ b/solution.py
@@ -272,10 +272,10 @@
     )
 
 
-same_side = [turn for turn in range(1, 16) if not turn & 4]
-other_side = [turn for turn in range(1, 16) if turn & 4]
-turn_order = list(range(1, 16))
-lead, lag, wait_lag = 5, 2, 6
+same_side = [8, 2, 10, 1, 9, 3, 11]
+other_side = [4, 12, 6, 14, 5, 13, 7, 15]
+turn_order = [4, 8, 6, 2, 12, 10, 5, 1, 14, 9, 13, 3, 7, 11, 15]
+lead, lag, wait_lag = 4, 2, 6
 
 
 def greet(place):
@@ -299,7 +299,8 @@
         half_out, half_in,
     ) = refs[3:]
     loads = [
-        pltpu.make_async_copy(conc_from, conc_ref, loaded.at[0]),
+        pltpu.make_async_copy(conc_from.at[0], conc_ref.at[0], loaded.at[0]),
+        pltpu.make_async_copy(conc_from.at[1], conc_ref.at[1], loaded.at[4]),
         pltpu.make_async_copy(y_from.at[1], y_ref.at[1], loaded.at[1]),
         pltpu.make_async_copy(x_from, x_ref, loaded.at[2]),
         pltpu.make_async_copy(y_from.at[0], y_ref.at[0], loaded.at[3]),
@@ -330,9 +331,11 @@
     quarter = slabs // 2
     met = greet(place)
 
-    def prepare(parity, wants_bulk):
+    def prepare(parity, wants_bulk, arriving=()):
         total = jnp.zeros((8, lanes), jnp.float32)
         for plane in range(planes):
+            for load in arriving[plane : plane + 1]:
+                load.wait()
             first = conc_ref[plane, :, :half]
             second = conc_ref[plane, :, half:]
             first_sq, second_sq = first * first, second * second
@@ -385,11 +388,15 @@
         return copies
 
     def spread(item):
-        @pl.when(shared(item) | is_inner)
+        @pl.when(shared(item))
+        def _():
+            start(copies_out(item, turn_order))
+
+        @pl.when(~shared(item) & is_inner)
         def _():
             start(copies_out(item, same_side))
 
-        @pl.when(shared(item) | ~is_inner)
+        @pl.when(~shared(item) & ~is_inner)
         def _():
             start(copies_out(item, other_side))
 
@@ -644,28 +651,35 @@
     special_at = chunks.index((0, 0)) // 2 * 3
     even_ref[...] = jnp.zeros_like(even_ref)
     odd_ref[...] = jnp.zeros_like(odd_ref)
-    loads[0].wait()
-    tile_ref[by_rows] = prepare(1, True)
-    loads[1].wait()
+    prepare(1, False, loads)
+    loads[2].wait()
     forward(1, 0, 0)
     met()
     spread(0)
-    start(spread_tile())
     forward(1, 1, 1)
-    loads[2].wait()
+    loads[3].wait()
     wide_table()
     lax.fori_loop(2, subs, lambda at, carry: forward(1, at, at), None)
-    for item in range(1, lead):
+    spread(1)
+    tile_ref[by_rows] = prepare(0, True)
+    start(spread_tile())
+    loads[4].wait()
+    lax.fori_loop(0, subs, lambda at, carry: forward(0, at, subs + at), None)
+
+    for item in range(2, lead):
         spread(item)
-    prepare(0, False)
-    loads[3].wait()
-    lax.fori_loop(0, subs, lambda at, carry: forward(0, at, subs + at), None)
 
     def one(item, carry):
         @pl.when(takes(item))
         def _():
             forth(item, members - 1).wait_recv()
 
+        @pl.when(item + lead < items)
+        def _():
+            spread(item + lead)
+
+        @pl.when(takes(item))
+        def _():
             @pl.when(item != special_at)
             def _():
                 middle(item, False)
@@ -676,10 +690,6 @@
 
             cross(item).start()
 
-        @pl.when(item + lead < items)
-        def _():
-            spread(item + lead)
-
         @pl.when(item == 0)
         def _():
             tile_all().wait_recv()
@@ -728,14 +738,25 @@
     far().wait_send()
 
 
-def combine_kernel(even_ref, odd_ref, out_ref):
+def combine_kernel(even_ref, odd_ref, out_to, out_ref, stored):
     planes, rows, full_y = out_ref.shape
     half = full_y // 2
+    step = rows // stored.shape[1]
+    stores = []
     for plane in range(planes):
-        even_rows = even_ref[plane * rows : (plane + 1) * rows, :]
-        odd_rows = odd_ref[plane * rows : (plane + 1) * rows, :]
-        out_ref[plane, :, :half] = even_rows + odd_rows
-        out_ref[plane, :, half:] = even_rows - odd_rows
+        for part in range(stored.shape[1]):
+            here = slice(part * step, (part + 1) * step)
+            at = slice(plane * rows + part * step, plane * rows + (part + 1) * step)
+            even_rows, odd_rows = even_ref[at, :], odd_ref[at, :]
+            out_ref[plane, here, :half] = even_rows + odd_rows
+            out_ref[plane, here, half:] = even_rows - odd_rows
+            store = pltpu.make_async_copy(
+                out_ref.at[plane, here], out_to.at[plane, here], stored.at[plane, part]
+            )
+            store.start()
+            stores.append(store)
+    for store in stores:
+        store.wait()
 
 
 def kernel_step(concentration):
@@ -786,7 +807,7 @@
             vmem(concentration.shape, f32),
             vmem(y_rows.shape, f32),
             vmem(x_rows.shape, f32),
-            dma((4,)),
+            dma((5,)),
             vmem((columns, half), bf16),
             vmem((columns, half), bf16),
             vmem((width, 2 * width), bf16),
@@ -816,7 +837,8 @@
         combine_kernel,
         out_shape=jax.ShapeDtypeStruct(concentration.shape, f32),
         in_specs=[in_vmem] * 2,
-        out_specs=in_vmem,
+        out_specs=pl.BlockSpec(memory_space=pltpu.HBM),
+        scratch_shapes=[vmem(concentration.shape, f32), dma((planes, 2))],
         compiler_params=pltpu.CompilerParams(vmem_limit_bytes=small_limit),
     )(even, odd)
     return (new_field, energy.reshape(()))

time: 127 us -> 125 us (0.984)
    pallas_call x1, Pallas kernels: 123 us -> 121 us  [kernel_step(): pl.pallas_call(functools.partial(step_kernel, cells, chunks), out_shape=(...]
where the time goes in v5:
time: 125 us
  Pallas kernels  123 us (98%)
  between operations  2.33 us (2%)
    pallas_call x1, Pallas kernels, kernel_step(): pl.pallas_call(functools.partial(step_kernel, cells, chunks), out_shape=(...  121 us

profile of v5, /device:TPU:0, one launch (start us, length us, event | category | flops | bytes accessed | tf_op | source)
XLA Modules:
  0.0 125.0 jit_solution(15752467886586042589)
XLA Ops:
  0.6 121.3 %shard_map.50 = (f32[256,1024]{1,0:T(8,128)S(1)}, f32[256,1024]{1,0:T(8,128)S(1)}, f32[1,1]{1,0:T(1,128)}) custom-call(f32[2,128,2048]{2,1,0:T(8,128)} %conc_from.1, f32[2,4,32,1024]{3,2,1,0:T(8,128)} %constant.4.clone.y_from, f32[120,512]{1,0:T(8,128)} %constant.5.clone.x_from), custom_call_target="tpu_custom_call" | custom-call | tf_op jit(solution)/shard_map/pallas_call | solution.py:797
  121.9 1.4 %shard_map.51 = f32[2,128,2048]{2,1,0:T(8,128)} custom-call(f32[256,1024]{1,0:T(8,128)S(1)} %get-tuple-element.5.even_ref, f32[256,1024]{1,0:T(8,128)S(1)} %get-tuple-element.6.odd_ref), custom_call_target="tpu_custom_call" | custom-call | tf_op jit(solution)/shard_map/pallas_call | solution.py:836

commit v6 on v5

--- a/solution.py
+++ b/solution.py
@@ -275,7 +275,7 @@
 same_side = [8, 2, 10, 1, 9, 3, 11]
 other_side = [4, 12, 6, 14, 5, 13, 7, 15]
 turn_order = [4, 8, 6, 2, 12, 10, 5, 1, 14, 9, 13, 3, 7, 11, 15]
-lead, lag, wait_lag = 4, 2, 6
+lead, lag, wait_lag = 4, 1, 6
 
 
 def greet(place):
@@ -838,7 +838,7 @@
         out_shape=jax.ShapeDtypeStruct(concentration.shape, f32),
         in_specs=[in_vmem] * 2,
         out_specs=pl.BlockSpec(memory_space=pltpu.HBM),
-        scratch_shapes=[vmem(concentration.shape, f32), dma((planes, 2))],
+        scratch_shapes=[vmem(concentration.shape, f32), dma((planes, 4))],
         compiler_params=pltpu.CompilerParams(vmem_limit_bytes=small_limit),
     )(even, odd)
     return (new_field, energy.reshape(()))

time: 125 us -> 127 us (1.016)
    pallas_call x1, Pallas kernels: 121 us -> 123 us  [kernel_step(): pl.pallas_call(functools.partial(step_kernel, cells, chunks), out_shape=(...]
where the time goes in v6:
time: 127 us
  Pallas kernels  124 us (98%)
  between operations  2.33 us (2%)
    pallas_call x1, Pallas kernels, kernel_step(): pl.pallas_call(functools.partial(step_kernel, cells, chunks), out_shape=(...  123 us

profile of v6, /device:TPU:0, one launch (start us, length us, event | category | flops | bytes accessed | tf_op | source)
XLA Modules:
  0.0 126.7 jit_solution(6458108644489416529)
XLA Ops:
  0.6 123.0 %shard_map.50 = (f32[256,1024]{1,0:T(8,128)S(1)}, f32[256,1024]{1,0:T(8,128)S(1)}, f32[1,1]{1,0:T(1,128)}) custom-call(f32[2,128,2048]{2,1,0:T(8,128)} %conc_from.1, f32[2,4,32,1024]{3,2,1,0:T(8,128)} %constant.4.clone.y_from, f32[120,512]{1,0:T(8,128)} %constant.5.clone.x_from), custom_call_target="tpu_custom_call" | custom-call | tf_op jit(solution)/shard_map/pallas_call | solution.py:797
  123.6 1.4 %shard_map.51 = f32[2,128,2048]{2,1,0:T(8,128)} custom-call(f32[256,1024]{1,0:T(8,128)S(1)} %get-tuple-element.5.even_ref, f32[256,1024]{1,0:T(8,128)S(1)} %get-tuple-element.6.odd_ref), custom_call_target="tpu_custom_call" | custom-call | tf_op jit(solution)/shard_map/pallas_call | solution.py:836
